TPU v7x, 32 devices: a whole 2x2x4 slice. The times are simulated.
32 devices in a mesh: hx: 4 (over y, x), hy: 4 (over z), tok: 2 (over core).
Axes of the slice: x: 2, y: 2, z: 4, core: 2. Of those that a mesh axis runs over, the one named last changes fastest.
Arguments:
- stream_in: bfloat16 [512, 4608], P('tok', ('hx', 'hy')), may hold values from -6 to 6
- before_gain: bfloat16 [4608], P(('hx', 'hy')), may hold values from 0.25 to 1.75
- after_gain: bfloat16 [4608], P(('hx', 'hy')), may hold values from 0.25 to 1.75
- feed_gain: bfloat16 [4608], P(('hx', 'hy')), may hold values from 0.25 to 1.75
- query_weight: bfloat16 [4608, 4096], P('tok', ('hx', 'hy')), may hold values from -1 to 1
- key_weight: bfloat16 [4608, 2048], P('tok', ('hx', 'hy')), may hold values from -64 to 64
- value_weight: bfloat16 [4608, 2048], P('tok', ('hx', 'hy')), may hold values from -0.09375 to 0.09375
- output_weight: bfloat16 [4096, 4608], P(('hx', 'hy'), 'tok'), may hold values from -0.09375 to 0.09375
- documents: int32 [512], P('tok'), may hold values from 0 to 7, never falling along the last dimension, each value on 1 to 128 neighbouring positions
Outputs:
- residual: bfloat16 [512, 4608], P('tok', ('hx', 'hy'))
- feed_input: bfloat16 [512, 4608], P('tok', ('hx', 'hy'))
Inputs may be any that keep to these rules, and one draw needn't show every extreme that they name: `documents`: ids never fall along the tokens; a document holds at most 128 tokens and may run across a sequence's end.
All inputs are finite; a program needn't handle non-finite values.
Results may differ from a plain program's by a relative error of at most 0.014.
The roundings to bfloat16 on the way count: a program that leaves them out, or rounds other values in their place, can miss the bound.
Values may be sent and summed in bfloat16 or wider, within the bound.
A program may use at most 64 MiB of HBM per device.

v0:
```python
import functools

import jax
import jax.numpy as jnp
import numpy as np
from jax import lax
from jax.experimental import pallas as pl
from jax.experimental.pallas import tpu as pltpu
from jax.sharding import PartitionSpec as P

D = 4608
QH = 32
HEAD = 128
LENGTH = 256
LANES = 128

epsilon = 1e-06
neg_big = -1e30
MESH = pl.DeviceIdType.MESH
F32 = jnp.float32
BF16 = jnp.bfloat16


def flip(index, mask):
    low = (index % 2 + mask % 2) % 2
    high = (index // 2 + mask // 2) % 2
    return low + 2 * high


def rope_tables():
    half = HEAD // 2
    frequency = (10000.0 ** (-np.arange(half, dtype=np.float32) / half)).astype(np.float32)
    angles = frequency[:, None] * np.arange(LENGTH, dtype=np.float32)[None, :]
    return np.stack([np.cos(angles), np.sin(angles)]).astype(np.float32)


def tall_row(row):
    return jnp.broadcast_to(row, (8, row.shape[1]))


def tall(block):
    return jnp.concatenate([block] * (LANES // block.shape[0]), axis=0).T


def kernel(
    paired,
    stream, docs, before, after_in, tables, wq, wk, wv, wo,
    branch_out, after_out, feed_out,
    slots, docs_v, before_v, after_v, tables_v, weights, out_weight, out_t, acc,
    terms, first_a, first_b, from_x, from_y, from_z,
    head, head_z, head_mid, head_plane, stats, stats_in, stats_mid, stats_zin,
    local_sem, weight_send, weight_recv, gather_send, gather_recv, reduce_send, reduce_recv,
    head_send, head_recv, stat_send, stat_recv,
):
    width, rows = stream.shape
    rest = width - rows
    a, b, c = lax.axis_index("hx"), lax.axis_index("hy"), lax.axis_index("tok")
    along_x, along_y, across = flip(a, 1), flip(a, 2), flip(a, 3)
    plane = (None, along_x, along_y, across)
    z_peers = [None] + [flip(b, j) for j in (1, 2, 3)]

    def offset_of(i, j):
        return pl.multiple_of((flip(a, i) * 4 + flip(b, j)) * width, 16)

    locals_ = [
        pltpu.make_async_copy(stream, slots.at[0], local_sem.at[0]),
        pltpu.make_async_copy(before, before_v, local_sem.at[1]),
        pltpu.make_async_copy(tables, tables_v, local_sem.at[2]),
        pltpu.make_async_copy(docs, docs_v, local_sem.at[7]),
        pltpu.make_async_copy(after_in, after_v, local_sem.at[8]),
    ]
    for copy in locals_:
        copy.start()
    wrows, qcols, kcols = wq.shape[0], wq.shape[1], wk.shape[1]
    shard = c if paired else 0
    start = pl.multiple_of(shard * wrows, 16)
    targets = [
        (wq, weights.at[pl.ds(start, wrows), pl.ds(0, qcols)]),
        (wk, weights.at[pl.ds(start, wrows), pl.ds(qcols, kcols)]),
        (wv, weights.at[pl.ds(start, wrows), pl.ds(qcols + kcols, kcols)]),
        (wo, out_weight.at[shard]),
    ]
    weight_local = [
        pltpu.make_async_copy(src, dst, local_sem.at[3 + k]) for k, (src, dst) in enumerate(targets)
    ]

    barrier = pltpu.get_barrier_semaphore()
    greet = [{"hx": along_x}, {"hx": along_y}, {"hx": across}]
    greet += [{"hy": z_peers[j]} for j in (1, 2, 3)]
    if paired:
        greet.append({"tok": 1 - c})
    for peer in greet:
        pl.semaphore_signal(barrier, inc=1, device_id=peer, device_id_type=MESH)
    for copy in weight_local:
        copy.start()

    row8 = lax.broadcasted_iota(jnp.int32, (8, rows), 0)
    locals_[0].wait()
    locals_[1].wait()
    own = slots[0].astype(F32)
    def padded(vector):
        wide_vector = vector.astype(F32)
        return jnp.concatenate([wide_vector, jnp.zeros((1, rows + LANES - vector.shape[1]), F32)], axis=1)

    before_row = padded(before_v[...])
    padded_tail = jnp.concatenate([before_row[:, rows:], jnp.zeros((1, rows - LANES), F32)], axis=1)
    head[...] = jnp.where(
        row8 == 0,
        jnp.sum(own * own, axis=0, keepdims=True),
        jnp.where(row8 == 1, before_row[:, :rows], jnp.where(row8 == 2, padded_tail, 0.0)),
    )
    pl.semaphore_wait(barrier, len(greet))

    def remote(src, dst, send, recv, peer):
        return pltpu.make_async_remote_copy(
            src_ref=src, dst_ref=dst, send_sem=send, recv_sem=recv, device_id=peer, device_id_type=MESH
        )

    half = width // 2
    top, bottom = pl.ds(0, half), pl.ds(half, half)

    def head_to_z(j):
        return remote(head, head_z.at[j - 1], head_send.at[j - 1], head_recv.at[j - 1], {"hy": z_peers[j]})

    def head_to_plane(i):
        return remote(head_mid, head_plane.at[i - 1], head_send.at[2 + i], head_recv.at[2 + i], {"hx": plane[i]})

    halves = (top, bottom)

    def gather_z(j):
        return remote(slots.at[0], slots.at[j], gather_send.at[j], gather_recv.at[j], {"hy": z_peers[j]})

    def gather_z3(h):
        part = halves[h]
        return remote(
            slots.at[0, part], slots.at[3, part], gather_send.at[20 + h], gather_recv.at[20 + h], {"hy": z_peers[3]}
        )

    def gather_x3(h):
        part = halves[h]
        return remote(
            slots.at[3, part], slots.at[7, part], gather_send.at[22 + h], gather_recv.at[22 + h], {"hx": along_x}
        )

    def gather_y3(h):
        part = halves[h]
        return remote(
            slots.at[3, part], slots.at[11, part], gather_send.at[24 + h], gather_recv.at[24 + h], {"hx": along_y}
        )

    def across_z(j, h):
        part, k = halves[h], (13 if j == 0 else 26) + h * 2
        return remote(
            slots.at[12 + j, part], slots.at[13 + j, part], gather_send.at[k], gather_recv.at[k], {"hy": z_peers[1]}
        )

    def gather_x(j):
        return remote(slots.at[j], slots.at[4 + j], gather_send.at[4 + j], gather_recv.at[4 + j], {"hx": along_x})

    def gather_y(j):
        return remote(slots.at[j], slots.at[8 + j], gather_send.at[8 + j], gather_recv.at[8 + j], {"hx": along_y})

    def relay_a(j):
        return remote(
            slots.at[4 + j, top], slots.at[12 + j, top], gather_send.at[12 + j], gather_recv.at[12 + j], {"hx": along_y}
        )

    def relay_b(j):
        return remote(
            slots.at[8 + j, bottom], slots.at[12 + j, bottom], gather_send.at[16 + j], gather_recv.at[16 + j], {"hx": along_x}
        )

    for j in (3, 2, 1):
        head_to_z(j).start()
    gather_x(0).start()
    gather_y(0).start()
    for j in (1, 2):
        gather_z(j).start()
    gather_z3(0).start()
    gather_z3(1).start()
    weight_remote = []
    if paired:
        weight_remote = [
            remote(src, dst, weight_send.at[k], weight_recv.at[k], {"tok": 1 - c})
            for k, (src, dst) in enumerate(targets)
        ]
        for copy in weight_remote:
            copy.start()

    def forward(j):
        gather_z(j).wait_recv()
        gather_x(j).start()
        gather_y(j).start()

    def relay(j):
        gather_x(j).wait_recv()
        relay_a(j).start()
        gather_y(j).wait_recv()
        relay_b(j).start()

    def spread(j):
        relay_a(j).wait_recv()
        across_z(j, 0).start()
        relay_b(j).wait_recv()
        across_z(j, 1).start()

    for j in (1, 2, 3):
        head_to_z(j).wait_recv()
    mains = [head[...]] + [head_z[j] for j in range(3)]
    total = mains[0] + mains[1] + mains[2] + mains[3]
    tails = jnp.zeros((1, rows), F32)
    for j in range(4):
        part = mains[j][2:3, :LANES]
        if j:
            part = pltpu.roll(tall_row(part), j * rest, 1)[0:1]
        tails = tails + jnp.concatenate([part, jnp.zeros((1, rows - LANES), F32)], axis=1)
    mid = jnp.where(row8 == 0, total[0:1], 0.0)
    for j in range(4):
        mid = jnp.where(row8 == 1 + j, mains[j][1:2], mid)
    head_mid[...] = jnp.where(row8 == 5, tails, mid)
    for i in (3, 1, 2):
        head_to_plane(i).start()
    forward(1)
    relay(0)
    for i in (1, 2, 3):
        head_to_plane(i).wait_recv()
    groups = [head_mid[...]] + [head_plane[i] for i in range(3)]
    first_sq = groups[0][0:1] + groups[1][0:1] + groups[2][0:1] + groups[3][0:1]
    first_scale = lax.rsqrt(first_sq / D + epsilon)
    gain_columns = tall(jnp.concatenate(groups, axis=0))
    for copy in weight_local[:3]:
        copy.wait()
    for copy in weight_remote[:3]:
        copy.wait_recv()

    def project(i, j):
        gain = jnp.concatenate(
            [gain_columns[:, 8 * i + 1 + j:8 * i + 2 + j], gain_columns[j * rest:(j + 1) * rest, 8 * i + 5:8 * i + 6]],
            axis=0,
        )
        normed = (slots[4 * i + j].astype(F32) * first_scale * gain).astype(BF16)
        part = lax.dot_general(
            weights[pl.ds(offset_of(i, j), width), :], normed, (((0,), (0,)), ((), ())), preferred_element_type=F32
        )
        if i == 0 and j == 0:
            acc[...] = part
        else:
            acc[...] += part

    shards, depth, columns = out_weight.shape

    def turn(k):
        span = 3 * LANES
        s, at = (k * span) // columns, (k * span) % columns
        out_t[k * span:(k + 1) * span, :] = out_weight[s, :, at:at + span].T

    project(0, 0)
    project(0, 1)
    forward(2)
    spread(0)
    project(0, 2)
    gather_x(1).wait_recv()
    gather_y(1).wait_recv()
    project(1, 0)
    project(2, 0)
    relay(2)
    for h in range(2):
        gather_z3(h).wait_recv()
        gather_x3(h).start()
        gather_y3(h).start()
    project(0, 3)
    project(1, 1)
    project(2, 1)
    project(3, 0)
    spread(2)
    weight_local[3].wait()
    for copy in weight_remote[3:]:
        copy.wait_recv()
    turns = D // (3 * LANES)
    for k in range(turns):
        turn(k)
    project(1, 2)
    project(2, 2)
    across_z(0, 0).wait_recv()
    across_z(0, 1).wait_recv()
    project(3, 1)
    project(3, 2)
    locals_[2].wait()
    locals_[3].wait()
    locals_[4].wait()
    doc_row = docs_v[...].astype(F32)
    after_row = padded(after_v[...])
    doc_col = tall(jnp.broadcast_to(doc_row, (8, rows)))[:, 0:1]
    after = tall(jnp.broadcast_to(after_row, (8, rows + LANES)))[:width, 0:1]
    s_index = lax.broadcasted_iota(jnp.int32, (LENGTH, LENGTH), 0)
    t_index = lax.broadcasted_iota(jnp.int32, (LENGTH, LENGTH), 1)
    for h in range(2):
        gather_x3(h).wait_recv()
        gather_y3(h).wait_recv()
    project(1, 3)
    project(2, 3)
    across_z(2, 0).wait_recv()
    across_z(2, 1).wait_recv()
    project(3, 3)

    cosine, sine = tables_v[0], tables_v[1]

    def rope(x):
        upper, lower = x[:HEAD // 2], x[HEAD // 2:]
        return jnp.concatenate([upper * cosine - lower * sine, lower * cosine + upper * sine], axis=0)

    query_heads, key_heads = qcols // HEAD, kcols // HEAD
    ratio = query_heads // key_heads
    allowed = (s_index <= t_index) & (doc_row == doc_col)
    attended = []
    for h in range(query_heads):
        kv = h // ratio
        query = (rope(acc[h * HEAD:(h + 1) * HEAD]) * (D / QH) ** (-0.5)).astype(BF16)
        key = rope(acc[qcols + kv * HEAD:qcols + (kv + 1) * HEAD]).astype(BF16)
        value = acc[qcols + kcols + kv * HEAD:qcols + kcols + (kv + 1) * HEAD].astype(BF16)
        scores = lax.dot_general(key, query, (((0,), (0,)), ((), ())), preferred_element_type=F32)
        best = jnp.max(jnp.where(allowed, scores, neg_big), axis=0, keepdims=True)
        soft = jnp.where(allowed, jnp.exp(scores - best), 0.0)
        mass = jnp.sum(soft, axis=0, keepdims=True)
        blended = jnp.dot(value, soft.astype(BF16), preferred_element_type=F32)
        attended.append((blended / mass).astype(BF16))
    attended = jnp.concatenate(attended, axis=0)

    def term(i, j):
        at = offset_of(i, j)
        terms[4 * i + j] = jnp.dot(out_t[pl.ds(at, width), :], attended, preferred_element_type=F32).astype(BF16)

    def diagonal_a(j):
        return remote(terms.at[12 + j, top], first_a.at[j], reduce_send.at[j], reduce_recv.at[j], {"hx": along_x})

    def diagonal_b(j):
        return remote(
            terms.at[12 + j, bottom], first_b.at[j], reduce_send.at[4 + j], reduce_recv.at[4 + j], {"hx": along_y}
        )

    def reduce_x(j):
        return remote(terms.at[4 + j], from_x.at[j], reduce_send.at[8 + j], reduce_recv.at[8 + j], {"hx": along_x})

    def reduce_y(j):
        return remote(terms.at[8 + j], from_y.at[j], reduce_send.at[12 + j], reduce_recv.at[12 + j], {"hx": along_y})

    def reduce_z(j):
        return remote(
            terms.at[j], from_z.at[j - 1], reduce_send.at[15 + j], reduce_recv.at[15 + j], {"hy": z_peers[j]}
        )

    def last_x(h):
        part = halves[h]
        return remote(
            terms.at[5, part], from_x.at[1, part], reduce_send.at[19 + h], reduce_recv.at[19 + h], {"hx": along_x}
        )

    def last_y(h):
        part = halves[h]
        return remote(
            terms.at[9, part], from_y.at[1, part], reduce_send.at[21 + h], reduce_recv.at[21 + h], {"hx": along_y}
        )

    def last_z(h):
        part = halves[h]
        return remote(
            terms.at[1, part], from_z.at[0, part], reduce_send.at[23 + h], reduce_recv.at[23 + h], {"hy": z_peers[1]}
        )

    def first(j):
        term(3, j)
        diagonal_a(j).start()
        diagonal_b(j).start()

    def second(j):
        term(2, j)
        term(1, j)
        diagonal_a(j).wait_recv()
        terms[8 + j, top, :] = (terms[8 + j, top, :].astype(F32) + first_a[j].astype(F32)).astype(BF16)
        if j == 1:
            last_y(0).start()
            last_y(1).start()
        else:
            reduce_y(j).start()
        diagonal_b(j).wait_recv()
        terms[4 + j, bottom, :] = (terms[4 + j, bottom, :].astype(F32) + first_b[j].astype(F32)).astype(BF16)
        if j == 1:
            last_x(0).start()
            last_x(1).start()
        else:
            reduce_x(j).start()

    def plane_sum(j):
        reduce_x(j).wait_recv()
        reduce_y(j).wait_recv()
        return terms[j].astype(F32) + from_x[j].astype(F32) + from_y[j].astype(F32)

    def third(j):
        terms[j] = plane_sum(j).astype(BF16)
        reduce_z(j).start()

    first(3)
    first(2)
    for j in (3, 2, 1, 0):
        term(0, j)
    second(3)
    first(1)
    second(2)
    first(0)
    second(1)
    third(3)
    second(0)
    third(2)
    for h in range(2):
        last_x(h).wait_recv()
        last_y(h).wait_recv()
        part = halves[h]
        summed = terms[1, part, :].astype(F32) + from_x[1, part, :].astype(F32) + from_y[1, part, :].astype(F32)
        terms[1, part, :] = summed.astype(BF16)
        last_z(h).start()
    mixed = plane_sum(0)
    for j in (3, 2, 1):
        if j == 1:
            last_z(0).wait_recv()
            last_z(1).wait_recv()
        else:
            reduce_z(j).wait_recv()
        mixed = mixed + from_z[j - 1].astype(F32)

    wide = slots[0].astype(F32)
    branch = mixed * after
    stats[...] = jnp.where(
        row8 == 0,
        jnp.sum(mixed * mixed, axis=0, keepdims=True),
        jnp.where(
            row8 == 1,
            jnp.sum(wide * branch, axis=0, keepdims=True),
            jnp.sum(branch * branch, axis=0, keepdims=True),
        ),
    )

    def stat_plane(i):
        return remote(stats, stats_in.at[i - 1], stat_send.at[i - 1], stat_recv.at[i - 1], {"hx": plane[i]})

    def stat_z(j):
        return remote(stats_mid, stats_zin.at[j - 1], stat_send.at[2 + j], stat_recv.at[2 + j], {"hy": z_peers[j]})

    for i in (3, 2, 1):
        stat_plane(i).start()
    for i in (1, 2, 3):
        stat_plane(i).wait_recv()
    stats_mid[...] = stats[...] + stats_in[0] + stats_in[1] + stats_in[2]
    for j in (3, 2, 1):
        stat_z(j).start()
    for j in (1, 2, 3):
        stat_z(j).wait_recv()
    summed = stats_mid[...] + stats_zin[0] + stats_zin[1] + stats_zin[2]
    after_scale = lax.rsqrt(summed[0:1] / D + epsilon)
    feed_sq = first_sq + 2.0 * after_scale * summed[1:2] + after_scale * after_scale * summed[2:3]
    feed_scale = lax.rsqrt(feed_sq / D + epsilon)
    branch_out[...] = branch
    after_out[...] = after_scale
    feed_out[...] = feed_scale

    for j in range(4):
        if j < 3:
            gather_x(j).wait_send()
            gather_y(j).wait_send()
        diagonal_a(j).wait_send()
        diagonal_b(j).wait_send()
        if j != 1:
            reduce_x(j).wait_send()
            reduce_y(j).wait_send()
    for j in (0, 2):
        relay_a(j).wait_send()
        relay_b(j).wait_send()
    for h in range(2):
        for copy in (gather_z3, gather_x3, gather_y3, last_x, last_y, last_z):
            copy(h).wait_send()
        across_z(0, h).wait_send()
        across_z(2, h).wait_send()
    for j in (1, 2, 3):
        head_to_z(j).wait_send()
        head_to_plane(j).wait_send()
        stat_plane(j).wait_send()
        stat_z(j).wait_send()
    for j in (1, 2):
        gather_z(j).wait_send()
    for j in (2, 3):
        reduce_z(j).wait_send()
    for copy in weight_remote:
        copy.wait_send()


def per_device(paired, stream_in, before_gain, after_gain, feed_gain, query_weight, key_weight, value_weight, output_weight, documents):
    rows, width = stream_in.shape
    if not paired:
        query_weight, key_weight, value_weight = (
            lax.all_gather(piece, "tok", axis=0, tiled=True) for piece in (query_weight, key_weight, value_weight)
        )
        output_weight = lax.all_gather(output_weight, "tok", axis=1, tiled=True)
    tables = jnp.asarray(rope_tables())
    qcols, kcols = query_weight.shape[1], key_weight.shape[1]
    shards = 2 if paired else 1
    depth = output_weight.shape[0]
    any_spec = pl.BlockSpec(memory_space=pl.ANY)
    vmem = pl.BlockSpec(memory_space=pltpu.VMEM)
    dma = pltpu.SemaphoreType.DMA
    block = (width, rows)
    branch, after_scale, feed_scale = pl.pallas_call(
        functools.partial(kernel, paired),
        out_shape=[jax.ShapeDtypeStruct(block, F32), jax.ShapeDtypeStruct((1, rows), F32), jax.ShapeDtypeStruct((1, rows), F32)],
        in_specs=[any_spec] * 9,
        out_specs=[vmem] * 3,
        scratch_shapes=[
            pltpu.VMEM((16,) + block, BF16),
            pltpu.VMEM((1, rows), jnp.int32),
            pltpu.VMEM((1, width), F32),
            pltpu.VMEM((1, width), F32),
            pltpu.VMEM((2, HEAD // 2, LENGTH), F32),
            pltpu.VMEM((D, qcols + 2 * kcols), BF16),
            pltpu.VMEM((shards, depth, output_weight.shape[1]), BF16),
            pltpu.VMEM((D, depth), BF16),
            pltpu.VMEM((qcols + 2 * kcols, rows), F32),
            pltpu.VMEM((16,) + block, BF16),
            pltpu.VMEM((4, width // 2, rows), BF16),
            pltpu.VMEM((4, width // 2, rows), BF16),
            pltpu.VMEM((4,) + block, BF16),
            pltpu.VMEM((4,) + block, BF16),
            pltpu.VMEM((3,) + block, BF16),
        ]
        + [pltpu.VMEM((8, rows), F32), pltpu.VMEM((3, 8, rows), F32)] * 4
        + [
            dma((9,)),
            dma((4,)),
            dma((4,)),
            dma((29,)),
            dma((29,)),
            dma((25,)),
            dma((25,)),
            dma((6,)),
            dma((6,)),
            dma((6,)),
            dma((6,)),
        ],
        compiler_params=pltpu.CompilerParams(
            collective_id=0, has_side_effects=True, vmem_limit_bytes=56 * 1024 * 1024
        ),
    )(
        stream_in.T,
        documents.reshape(1, rows),
        before_gain.astype(F32).reshape(1, width),
        after_gain.astype(F32).reshape(1, width),
        tables,
        query_weight,
        key_weight,
        value_weight,
        output_weight,
    )
    after_scale, feed_scale = after_scale.reshape(rows, 1), feed_scale.reshape(rows, 1)
    wide = stream_in.astype(F32)
    residual = (wide + branch.T * after_scale).astype(BF16)
    feed_input = (residual.astype(F32) * feed_scale * feed_gain.astype(F32)[None, :]).astype(BF16)
    return residual, feed_input


def solution(mesh):
    both = ("hx", "hy")
    in_specs = (
        P("tok", both),
        P(both),
        P(both),
        P(both),
        P("tok", both),
        P("tok", both),
        P("tok", both),
        P(both, "tok"),
        P("tok"),
    )
    out_specs = (P("tok", both), P("tok", both))
    paired = mesh.shape["tok"] == 2
    return jax.shard_map(
        functools.partial(per_device, paired), mesh=mesh, in_specs=in_specs, out_specs=out_specs, check_vma=False
    )
```

profile of v0, /device:TPU:0, one launch (start us, length us, event | category | flops | bytes accessed | tf_op | source)
XLA Modules:
  0.0 69.0 jit_solution(4129281951940861425)
XLA Ops:
  0.6 1.2 %reshape.28.before = f32[1,288]{1,0:T(1,128)} reshape(bf16[288]{0:T(512)(128)(2,1)} %param.11) | data formatting | bytes 1728 | tf_op jit(solution)/shard_map/reshape | solution.py:552
  1.9 1.2 %reshape.30.after_in = f32[1,288]{1,0:T(1,128)} reshape(bf16[288]{0:T(512)(128)(2,1)} %param.12) | data formatting | bytes 1728 | tf_op jit(solution)/shard_map/reshape | solution.py:553
  3.1 0.7 convert_element_type.20
  3.8 0.0 copy-start
  3.8 63.4 %shard_map.113 = (f32[288,256]{1,0:T(8,128)}, f32[1,256]{1,0:T(1,128)}, f32[1,256]{1,0:T(1,128)}) custom-call(bf16[288,256]{1,0:T(8,128)(2,1)} %bitcast.9, s32[1,256]{1,0:T(1,128)} %bitcast.10, f32[1,288]{1,0:T(1,128)} %reshape.28.before, f32[1,288]{1,0:T(1,128)} %reshape.30.after_in, f32[2,64,256]{2,1,0:T(8,128)} %constant.2.clone.tables, ...), custom_call_target="tpu_custom_call" | custom-call | tf_op jit(solution)/shard_map/pallas_call | solution.py:510
  67.2 0.0 copy-done
  67.2 1.7 %multiply_convert_fusion = (bf16[256,288]{0,1:T(8,128)(2,1)}, bf16[256,288]{0,1:T(8,128)(2,1)}) fusion(f32[288]{0:T(512)S(1)} %convert_element_type.20, f32[256]{0:T(256)} %bitcast.12, f32[288,256]{1,0:T(8,128)} %get-tuple-element.5, f32[256]{0:T(256)} %bitcast.11, bf16[256,288]{0,1:T(8,128)(2,1)S(1)} %copy-done), kind=kLoop, calls=%fused_computation.2 | loop fusion | flops 589824 | bytes 740480 | tf_op jit(solution)/shard_map/convert_element_type | solution.py:563
Async XLA Ops:
  3.8 63.4 %copy-start = (bf16[256,288]{0,1:T(8,128)(2,1)S(1)}, bf16[256,288]{0,1:T(8,128)(2,1)}, u32[]{:S(2)}) copy-start(bf16[256,288]{0,1:T(8,128)(2,1)} %param.10) | copy-start | bytes 442372
where the time goes:
time: 69.1 us; the launch traced here: 69 us
  Pallas kernels  63.4 us (92%)
  local copies, waits for them, and re-layouts  2.49 us (4%)
  other arithmetic  2.41 us (3%)
    pallas_call x1, Pallas kernels, per_device(): pl.pallas_call(functools.partial(kernel, paired), out_shape=[jax.ShapeDty...  63.4 us
    convert_element_type x1, other arithmetic, per_device(): (residual.astype(F32) * feed_scale * feed_gain.astype(F32)[None, :]).asty...  1.73 us

commit v1 on v0

v1 whole, which is shorter than its diff:
```python
import functools

import jax
import jax.numpy as jnp
import numpy as np
from jax import lax
from jax.experimental import pallas as pl
from jax.experimental.pallas import tpu as pltpu
from jax.sharding import PartitionSpec as P

D = 4608
QH = 32
HEAD = 128
LENGTH = 256
LANES = 128

epsilon = 1e-06
neg_big = -1e30
MESH = pl.DeviceIdType.MESH
F32 = jnp.float32
BF16 = jnp.bfloat16


GATHER = {
    "A": ("", "z1", "z2", "z3", "x", "x", "x", "z1", "y", "y", "y", "z1", "x", "z1", "x", "x"),
    "B": ("", "z1", "z2", "z3", "x", "z1", "z1", "x", "y", "y", "y", "y", "y", "y", "x", "x"),
}
REDUCE = {
    "A": ("", "z1", "z2", "z3", "z1", "x", "x", "z1", "y", "y", "y", "y", "x", "y", "x", "z1"),
    "B": ("", "z1", "z2", "z3", "z1", "x", "x", "x", "y", "y", "y", "y", "x", "z1", "y", "x"),
}
ORDER = (
    "hz", "s10B", "s02A", "s20B", "s20A", "s01A", "s03B", "hw", "hm", "s10A",
    "s30A", "s22A", "s11B", "s02B", "s01B", "s12A", "head", "p10A", "s21A", "s11A",
    "s23B", "s23A", "p00B", "s31A", "p20A", "s13B", "s32A", "p02A", "p11B", "s03A",
    "s31B", "p11A", "s22B", "p21A", "p10B", "s33B", "s21B", "p22A", "p12A", "p03B",
    "turn", "p13B", "s33A", "p01B", "s30B", "p00A", "p02B", "s13A", "p30A", "p32A",
    "p01A", "p23B", "s12B", "s32B", "p31A", "p33B", "p23A", "p20B", "p22B", "p21B",
    "p31B", "p33A", "p03A", "p13A", "aA", "t33A", "u33A", "p30B", "t23A", "u23A",
    "p32B", "p12B", "aB", "t32B", "t10A", "u10A", "u32B", "t21B", "t13A", "t13B",
    "t12A", "u13B", "t32A", "t22B", "t22A", "t33B", "t23B", "t31A", "t03A", "t01A",
    "t31B", "t21A", "t10B", "t03B", "u31A", "u10B", "t12B", "t00A", "t30A", "t01B",
    "u33B", "u22B", "u21B", "t02A", "t00B", "t02B", "u13A", "u12B", "u31B", "u03A",
    "u32A", "u21A", "t11A", "u23B", "u11A", "u02B", "u12A", "u30A", "t20A", "t30B",
    "t20B", "t11B", "u22A", "u11B", "u01A", "u03B", "u30B", "u02A", "u20A", "u01B",
    "u20B", "finA", "finB",
)


def flip(index, mask):
    low = (index % 2 + mask % 2) % 2
    high = (index // 2 + mask // 2) % 2
    return low + 2 * high


def rope_tables():
    half = HEAD // 2
    frequency = (10000.0 ** (-np.arange(half, dtype=np.float32) / half)).astype(np.float32)
    angles = frequency[:, None] * np.arange(LENGTH, dtype=np.float32)[None, :]
    return np.stack([np.cos(angles), np.sin(angles)]).astype(np.float32)


def tall_row(row):
    return jnp.broadcast_to(row, (8, row.shape[1]))


def tall(block):
    return jnp.concatenate([block] * (LANES // block.shape[0]), axis=0).T


def parent(block, link):
    i, j = block
    if link == "x":
        return i ^ 1, j
    if link == "y":
        return i ^ 2, j
    return i, j ^ int(link[1])


def kernel(
    paired,
    stream, docs, before, after_in, feed_in, tables, wq, wk, wv, wo,
    outs,
    slots, docs_v, before_v, after_v, feed_v, branch_v, tables_v, weights, out_weight, out_t, acc, keys, values, attended,
    terms, shares, head, head_z, head_mid, head_plane, stats, stats_in, stats_mid, stats_zin,
    local_sem, weight_send, weight_recv, gather_send, gather_recv, reduce_send, reduce_recv,
    head_send, head_recv, stat_send, stat_recv,
):
    width, rows = stream.shape
    rest = width - rows
    span = rows // 2
    a, b, c = lax.axis_index("hx"), lax.axis_index("hy"), lax.axis_index("tok")
    along_x, along_y, across = flip(a, 1), flip(a, 2), flip(a, 3)
    plane = (None, along_x, along_y, across)
    z_peers = [None] + [flip(b, j) for j in (1, 2, 3)]
    peers = {"x": {"hx": along_x}, "y": {"hx": along_y}}
    for j in (1, 2, 3):
        peers["z" + str(j)] = {"hy": z_peers[j]}

    def offset_of(i, j):
        return pl.multiple_of((flip(a, i) * 4 + flip(b, j)) * width, 16)

    locals_ = [
        pltpu.make_async_copy(stream.at[:, pl.ds(0, span)], slots.at[0, 0], local_sem.at[0]),
        pltpu.make_async_copy(stream.at[:, pl.ds(span, span)], slots.at[1, 0], local_sem.at[9]),
        pltpu.make_async_copy(before, before_v, local_sem.at[1]),
        pltpu.make_async_copy(tables, tables_v, local_sem.at[2]),
        pltpu.make_async_copy(docs, docs_v, local_sem.at[7]),
        pltpu.make_async_copy(after_in, after_v, local_sem.at[8]),
        pltpu.make_async_copy(feed_in, feed_v, local_sem.at[10]),
    ]
    for copy in locals_:
        copy.start()
    wrows, qcols, kcols = wq.shape[0], wq.shape[1], wk.shape[1]
    shard = c if paired else 0
    start = pl.multiple_of(shard * wrows, 16)
    targets = [
        (wq, weights.at[pl.ds(start, wrows), pl.ds(0, qcols)]),
        (wk, weights.at[pl.ds(start, wrows), pl.ds(qcols, kcols)]),
        (wv, weights.at[pl.ds(start, wrows), pl.ds(qcols + kcols, kcols)]),
        (wo, out_weight.at[shard]),
    ]
    weight_local = [
        pltpu.make_async_copy(src, dst, local_sem.at[3 + k]) for k, (src, dst) in enumerate(targets)
    ]

    barrier = pltpu.get_barrier_semaphore()
    greet = [{"hx": along_x}, {"hx": along_y}, {"hx": across}]
    greet += [{"hy": z_peers[j]} for j in (1, 2, 3)]
    if paired:
        greet.append({"tok": 1 - c})
    for peer in greet:
        pl.semaphore_signal(barrier, inc=1, device_id=peer, device_id_type=MESH)
    for copy in weight_local:
        copy.start()

    row8 = lax.broadcasted_iota(jnp.int32, (8, rows), 0)
    for copy in locals_[:3]:
        copy.wait()
    own = jnp.concatenate([slots[0, 0], slots[1, 0]], axis=1).astype(F32)

    def padded(vector):
        wide_vector = vector.astype(F32).reshape(1, width)
        return jnp.concatenate([wide_vector, jnp.zeros((1, rows + LANES - width), F32)], axis=1)

    before_row = padded(before_v[...])
    padded_tail = jnp.concatenate([before_row[:, rows:], jnp.zeros((1, rows - LANES), F32)], axis=1)
    head[...] = jnp.where(
        row8 == 0,
        jnp.sum(own * own, axis=0, keepdims=True),
        jnp.where(row8 == 1, before_row[:, :rows], jnp.where(row8 == 2, padded_tail, 0.0)),
    )
    pl.semaphore_wait(barrier, len(greet))

    def remote(src, dst, send, recv, peer):
        return pltpu.make_async_remote_copy(
            src_ref=src, dst_ref=dst, send_sem=send, recv_sem=recv, device_id=peer, device_id_type=MESH
        )

    def head_to_z(j):
        return remote(head, head_z.at[j - 1], head_send.at[j - 1], head_recv.at[j - 1], {"hy": z_peers[j]})

    def head_to_plane(i):
        return remote(head_mid, head_plane.at[i - 1], head_send.at[2 + i], head_recv.at[2 + i], {"hx": plane[i]})

    def gather(block, h):
        link = GATHER["AB"[h]][4 * block[0] + block[1]]
        origin = parent(block, link)
        k = 4 * block[0] + block[1]
        return remote(
            slots.at[h, 4 * origin[0] + origin[1]], slots.at[h, k], gather_send.at[h, k], gather_recv.at[h, k], peers[link]
        )

    def share(block, h):
        k = 4 * block[0] + block[1]
        link = REDUCE["AB"[h]][k]
        return remote(terms.at[h, k], shares.at[h, k], reduce_send.at[h, k], reduce_recv.at[h, k], peers[link])

    blocks = [(i, j) for i in range(4) for j in range(4)]
    children = {(h, block): [] for h in range(2) for block in blocks}
    for h in range(2):
        for block in blocks[1:]:
            link = REDUCE["AB"[h]][4 * block[0] + block[1]]
            children[h, parent(block, link)].append(block)

    weight_remote = []
    if paired:
        weight_remote = [
            remote(src, dst, weight_send.at[k], weight_recv.at[k], {"tok": 1 - c})
            for k, (src, dst) in enumerate(targets)
        ]
    state = {}
    arrived = set()

    def await_gather(block, h):
        if block != (0, 0) and ("g", block, h) not in arrived:
            arrived.add(("g", block, h))
            gather(block, h).wait_recv()

    def send_heads():
        for j in (3, 2, 1):
            head_to_z(j).start()

    def send_weights():
        for copy in weight_remote:
            copy.start()

    def relay_heads():
        for j in (1, 2, 3):
            head_to_z(j).wait_recv()
        mains = [head[...]] + [head_z[j] for j in range(3)]
        total = mains[0] + mains[1] + mains[2] + mains[3]
        tails = jnp.zeros((1, rows), F32)
        for j in range(4):
            part = mains[j][2:3, :LANES]
            if j:
                part = pltpu.roll(tall_row(part), j * rest, 1)[0:1]
            tails = tails + jnp.concatenate([part, jnp.zeros((1, rows - LANES), F32)], axis=1)
        mid = jnp.where(row8 == 0, total[0:1], 0.0)
        for j in range(4):
            mid = jnp.where(row8 == 1 + j, mains[j][1:2], mid)
        head_mid[...] = jnp.where(row8 == 5, tails, mid)
        for i in (3, 1, 2):
            head_to_plane(i).start()

    def use_heads():
        for i in (1, 2, 3):
            head_to_plane(i).wait_recv()
        groups = [head_mid[...]] + [head_plane[i] for i in range(3)]
        state["first_sq"] = groups[0][0:1] + groups[1][0:1] + groups[2][0:1] + groups[3][0:1]
        state["first_scale"] = lax.rsqrt(state["first_sq"] / D + epsilon)
        state["gain_columns"] = tall(jnp.concatenate(groups, axis=0))
        for copy in weight_local[:3]:
            copy.wait()
        for copy in weight_remote[:3]:
            copy.wait_recv()

    def project(block, h):
        await_gather(block, h)
        i, j = block
        gain_columns = state["gain_columns"]
        gain = jnp.concatenate(
            [gain_columns[:, 8 * i + 1 + j:8 * i + 2 + j], gain_columns[j * rest:(j + 1) * rest, 8 * i + 5:8 * i + 6]],
            axis=0,
        )
        scale = state["first_scale"][:, h * span:(h + 1) * span]
        normed = (slots[h, 4 * i + j].astype(F32) * scale * gain).astype(BF16)
        part = lax.dot_general(
            weights[pl.ds(offset_of(i, j), width), :], normed, (((0,), (0,)), ((), ())), preferred_element_type=F32
        )
        if ("p", h) not in arrived:
            arrived.add(("p", h))
            acc[h] = part
        else:
            acc[h] += part

    shards, depth, columns = out_weight.shape

    def turn():
        weight_local[3].wait()
        for copy in weight_remote[3:]:
            copy.wait_recv()
        for copy in locals_[3:]:
            copy.wait()
        step = 3 * LANES
        for k in range(D // step):
            s, at = (k * step) // columns, (k * step) % columns
            out_t[k * step:(k + 1) * step, :] = out_weight[s, :, at:at + step].T
        doc_row = docs_v[...].astype(F32)
        after_row = padded(after_v[...])
        state["doc_row"] = doc_row
        state["doc_col"] = tall(jnp.broadcast_to(doc_row, (8, rows)))[:, 0:1]
        feed_row = padded(feed_v[...])
        state["feed"] = tall(jnp.broadcast_to(feed_row, (8, rows + LANES)))[:width, 0:1]
        state["after"] = tall(jnp.broadcast_to(after_row, (8, rows + LANES)))[:width, 0:1]

    query_heads, key_heads = qcols // HEAD, kcols // HEAD
    ratio = query_heads // key_heads

    def attend(h):
        lanes = slice(h * span, (h + 1) * span)
        seen = (h + 1) * span
        cosine, sine = tables_v[0, :, lanes], tables_v[1, :, lanes]

        def rope(x):
            upper, lower = x[:HEAD // 2], x[HEAD // 2:]
            return jnp.concatenate([upper * cosine - lower * sine, lower * cosine + upper * sine], axis=0)

        for kv in range(key_heads):
            keys[kv, :, lanes] = rope(acc[h, qcols + kv * HEAD:qcols + (kv + 1) * HEAD]).astype(BF16)
            values[kv, :, lanes] = acc[h, qcols + kcols + kv * HEAD:qcols + kcols + (kv + 1) * HEAD].astype(BF16)
        s_index = lax.broadcasted_iota(jnp.int32, (seen, span), 0)
        t_index = lax.broadcasted_iota(jnp.int32, (seen, span), 1) + h * span
        allowed = (s_index <= t_index) & (state["doc_row"][:, lanes] == state["doc_col"][:seen])
        for q in range(query_heads):
            query = (rope(acc[h, q * HEAD:(q + 1) * HEAD]) * (D / QH) ** (-0.5)).astype(BF16)
            key, value = keys[q // ratio, :, :seen], values[q // ratio, :, :seen]
            scores = lax.dot_general(key, query, (((0,), (0,)), ((), ())), preferred_element_type=F32)
            best = jnp.max(jnp.where(allowed, scores, neg_big), axis=0, keepdims=True)
            soft = jnp.where(allowed, jnp.exp(scores - best), 0.0)
            mass = jnp.sum(soft, axis=0, keepdims=True)
            blended = jnp.dot(value, soft.astype(BF16), preferred_element_type=F32)
            attended[h, q * HEAD:(q + 1) * HEAD, :] = (blended / mass).astype(BF16)

    def term(block, h):
        at = offset_of(*block)
        terms[h, 4 * block[0] + block[1]] = jnp.dot(
            out_t[pl.ds(at, width), :], attended[h], preferred_element_type=F32
        ).astype(BF16)

    def collect(block, h):
        for child in children[h, block]:
            share(child, h).wait_recv()
        total = terms[h, 4 * block[0] + block[1]].astype(F32)
        for child in children[h, block]:
            total = total + shares[h, 4 * child[0] + child[1]].astype(F32)
        return total

    def pass_on(block, h):
        if children[h, block]:
            terms[h, 4 * block[0] + block[1]] = collect(block, h).astype(BF16)
        share(block, h).start()

    def finish(h):
        mixed = collect((0, 0), h)
        lanes = slice(h * span, (h + 1) * span)
        wide = slots[h, 0].astype(F32)
        branch = mixed * state["after"]
        narrow = row8[:, :span]
        stats[:, lanes] = jnp.where(
            narrow == 0,
            jnp.sum(mixed * mixed, axis=0, keepdims=True),
            jnp.where(
                narrow == 1,
                jnp.sum(wide * branch, axis=0, keepdims=True),
                jnp.sum(branch * branch, axis=0, keepdims=True),
            ),
        )
        branch_v[:, lanes] = branch

    for task in ORDER:
        if task == "hz":
            send_heads()
        elif task == "hw":
            send_weights()
        elif task == "hm":
            relay_heads()
        elif task == "head":
            use_heads()
        elif task == "turn":
            turn()
        elif task[:3] == "fin":
            finish("AB".index(task[3]))
        elif task[0] == "a":
            attend("AB".index(task[1]))
        else:
            block, h = (int(task[1]), int(task[2])), "AB".index(task[3])
            if task[0] == "s":
                copy = gather(block, h)
                await_gather(parent(block, GATHER["AB"[h]][4 * block[0] + block[1]]), h)
                copy.start()
            elif task[0] == "p":
                project(block, h)
            elif task[0] == "t":
                term(block, h)
            elif task[0] == "u":
                pass_on(block, h)

    def stat_plane(i):
        return remote(stats, stats_in.at[i - 1], stat_send.at[i - 1], stat_recv.at[i - 1], {"hx": plane[i]})

    def stat_z(j):
        return remote(stats_mid, stats_zin.at[j - 1], stat_send.at[2 + j], stat_recv.at[2 + j], {"hy": z_peers[j]})

    for i in (3, 2, 1):
        stat_plane(i).start()
    for i in (1, 2, 3):
        stat_plane(i).wait_recv()
    stats_mid[...] = stats[...] + stats_in[0] + stats_in[1] + stats_in[2]
    for j in (3, 2, 1):
        stat_z(j).start()
    for h in range(2):
        for block in blocks[1:]:
            gather(block, h).wait_send()
            share(block, h).wait_send()
    for j in (1, 2, 3):
        head_to_z(j).wait_send()
        head_to_plane(j).wait_send()
        stat_plane(j).wait_send()
    for copy in weight_remote:
        copy.wait_send()
    for j in (1, 2, 3):
        stat_z(j).wait_recv()
    summed = stats_mid[...] + stats_zin[0] + stats_zin[1] + stats_zin[2]
    after_scale = lax.rsqrt(summed[0:1] / D + epsilon)
    feed_sq = state["first_sq"] + 2.0 * after_scale * summed[1:2] + after_scale * after_scale * summed[2:3]
    feed_scale = lax.rsqrt(feed_sq / D + epsilon)
    for h in range(2):
        lanes = slice(h * span, (h + 1) * span)
        residual = (slots[h, 0].astype(F32) + branch_v[:, lanes] * after_scale[:, lanes]).astype(BF16)
        outs[0, :, lanes] = residual
        outs[1, :, lanes] = (residual.astype(F32) * feed_scale[:, lanes] * state["feed"]).astype(BF16)
    for j in (1, 2, 3):
        stat_z(j).wait_send()


def per_device(paired, stream_in, before_gain, after_gain, feed_gain, query_weight, key_weight, value_weight, output_weight, documents):
    rows, width = stream_in.shape
    if not paired:
        query_weight, key_weight, value_weight = (
            lax.all_gather(piece, "tok", axis=0, tiled=True) for piece in (query_weight, key_weight, value_weight)
        )
        output_weight = lax.all_gather(output_weight, "tok", axis=1, tiled=True)
    tables = jnp.asarray(rope_tables())
    qcols, kcols = query_weight.shape[1], key_weight.shape[1]
    shards = 2 if paired else 1
    depth = output_weight.shape[0]
    any_spec = pl.BlockSpec(memory_space=pl.ANY)
    vmem = pl.BlockSpec(memory_space=pltpu.VMEM)
    dma = pltpu.SemaphoreType.DMA
    block, piece = (width, rows), (width, rows // 2)
    both = pl.pallas_call(
        functools.partial(kernel, paired),
        out_shape=jax.ShapeDtypeStruct((2,) + block, BF16),
        in_specs=[any_spec] * 10,
        out_specs=vmem,
        scratch_shapes=[
            pltpu.VMEM((2, 16) + piece, BF16),
            pltpu.VMEM((1, rows), jnp.int32),
            pltpu.VMEM((width,), BF16),
            pltpu.VMEM((width,), BF16),
            pltpu.VMEM((width,), BF16),
            pltpu.VMEM(block, F32),
            pltpu.VMEM((2, HEAD // 2, LENGTH), F32),
            pltpu.VMEM((D, qcols + 2 * kcols), BF16),
            pltpu.VMEM((shards, depth, output_weight.shape[1]), BF16),
            pltpu.VMEM((D, depth), BF16),
            pltpu.VMEM((2, qcols + 2 * kcols, rows // 2), F32),
            pltpu.VMEM((kcols // HEAD, HEAD, rows), BF16),
            pltpu.VMEM((kcols // HEAD, HEAD, rows), BF16),
            pltpu.VMEM((2, qcols, rows // 2), BF16),
            pltpu.VMEM((2, 16) + piece, BF16),
            pltpu.VMEM((2, 16) + piece, BF16),
        ]
        + [pltpu.VMEM((8, rows), F32), pltpu.VMEM((3, 8, rows), F32)] * 4
        + [
            dma((11,)),
            dma((4,)),
            dma((4,)),
            dma((2, 16)),
            dma((2, 16)),
            dma((2, 16)),
            dma((2, 16)),
            dma((6,)),
            dma((6,)),
            dma((6,)),
            dma((6,)),
        ],
        compiler_params=pltpu.CompilerParams(
            collective_id=0, has_side_effects=True, vmem_limit_bytes=56 * 1024 * 1024
        ),
    )(
        stream_in.T,
        documents.reshape(1, rows),
        before_gain,
        after_gain,
        feed_gain,
        tables,
        query_weight,
        key_weight,
        value_weight,
        output_weight,
    )
    return both[0].T, both[1].T


def solution(mesh):
    both = ("hx", "hy")
    in_specs = (
        P("tok", both),
        P(both),
        P(both),
        P(both),
        P("tok", both),
        P("tok", both),
        P("tok", both),
        P(both, "tok"),
        P("tok"),
    )
    out_specs = (P("tok", both), P("tok", both))
    paired = mesh.shape["tok"] == 2
    return jax.shard_map(
        functools.partial(per_device, paired), mesh=mesh, in_specs=in_specs, out_specs=out_specs, check_vma=False
    )
```

time: 69.1 us -> 58.4 us (0.85)
  Pallas kernels: 63.4 us -> 55.9 us
  other arithmetic: 2.41 us -> 0 us
  local copies, waits for them, and re-layouts: 2.49 us -> 1.71 us
    pallas_call x1, Pallas kernels: 63.4 us -> 55.9 us  [per_device(): pl.pallas_call(functools.partial(kernel, paired), out_shape=jax.ShapeDtyp...]
    reshape x2 -> x0, local copies, waits for them, and re-layouts: 2.49 us -> none  [the longest x1 1.24 us: per_device(): before_gain.astype(F32).reshape(1, width)]
    convert_element_type x2 -> x0, other arithmetic: 2.41 us -> none  [the longest x1 1.73 us: per_device(): (residual.astype(F32) * feed_scale * feed_gain.astype(F32)[None, :]).asty...]
    transpose x0 -> x1, local copies, waits for them, and re-layouts: none -> 1.71 us  [per_device(): return (both[0].T, both[1].T)]
where the time goes in v1:
time: 58.4 us; the launch traced here: 58.3 us
  Pallas kernels  55.9 us (96%)
  local copies, waits for them, and re-layouts  1.71 us (3%)
  between operations  0.64 us (1%)
    pallas_call x1, Pallas kernels, per_device(): pl.pallas_call(functools.partial(kernel, paired), out_shape=jax.ShapeDtyp...  55.9 us
    transpose x1, local copies, waits for them, and re-layouts, per_device(): return (both[0].T, both[1].T)  1.71 us

profile of v1, /device:TPU:0, one launch (start us, length us, event | category | flops | bytes accessed | tf_op | source)
XLA Modules:
  0.0 58.3 jit_solution(13249197569198999815)
XLA Ops:
  0.6 55.9 %shard_map.113 = bf16[2,288,256]{2,1,0:T(8,128)(2,1)} custom-call(bf16[288,256]{1,0:T(8,128)(2,1)} %bitcast.10, s32[1,256]{1,0:T(1,128)} %bitcast.11, bf16[288]{0:T(512)(128)(2,1)} %before.1, bf16[288]{0:T(512)(128)(2,1)} %after_in.1, bf16[288]{0:T(512)(128)(2,1)} %feed_in.1, f32[2,64,256]{2,1,0:T(8,128)} %constant.2.clone.tables, bf16[2304,256]{1,0:T(8,128)(2,1)} %wq.1, ...), custom_call_target="tpu_custom_call" | custom-call | tf_op jit(solution)/shard_map/pallas_call | solution.py:422
  56.5 1.7 %slice_bitcast_fusion = (bf16[256,288]{0,1:T(8,128)(2,1)}, bf16[256,288]{0,1:T(8,128)(2,1)}) fusion(bf16[2,288,256]{2,1,0:T(8,128)(2,1)} %shard_map.113), kind=kLoop, calls=%fused_computation | loop fusion | bytes 589824 | tf_op jit(solution)/shard_map/transpose | solution.py:474

commit v2 on v1

--- a/solution.py
+++ b/solution.py
@@ -22,28 +22,24 @@
 
 
 GATHER = {
-    "A": ("", "z1", "z2", "z3", "x", "x", "x", "z1", "y", "y", "y", "z1", "x", "z1", "x", "x"),
-    "B": ("", "z1", "z2", "z3", "x", "z1", "z1", "x", "y", "y", "y", "y", "y", "y", "x", "x"),
+    "A": ("", "z1", "z1", "z3", "x", "x", "z1", "x", "y", "y", "y", "y", "d", "z1", "z1", "d"),
+    "B": ("", "z1", "z2", "z1", "x", "x", "x", "z1", "y", "y", "y", "y", "x", "z1", "x", "d"),
 }
 REDUCE = {
-    "A": ("", "z1", "z2", "z3", "z1", "x", "x", "z1", "y", "y", "y", "y", "x", "y", "x", "z1"),
-    "B": ("", "z1", "z2", "z3", "z1", "x", "x", "x", "y", "y", "y", "y", "x", "z1", "y", "x"),
+    "A": ("", "z1", "z2", "z3", "x", "x", "x", "z1", "y", "y", "y", "y", "x", "z1", "y", "x"),
+    "B": ("", "z1", "z2", "z1", "x", "x", "x", "x", "y", "y", "y", "z1", "d", "z1", "y", "x"),
 }
 ORDER = (
-    "hz", "s10B", "s02A", "s20B", "s20A", "s01A", "s03B", "hw", "hm", "s10A",
-    "s30A", "s22A", "s11B", "s02B", "s01B", "s12A", "head", "p10A", "s21A", "s11A",
-    "s23B", "s23A", "p00B", "s31A", "p20A", "s13B", "s32A", "p02A", "p11B", "s03A",
-    "s31B", "p11A", "s22B", "p21A", "p10B", "s33B", "s21B", "p22A", "p12A", "p03B",
-    "turn", "p13B", "s33A", "p01B", "s30B", "p00A", "p02B", "s13A", "p30A", "p32A",
-    "p01A", "p23B", "s12B", "s32B", "p31A", "p33B", "p23A", "p20B", "p22B", "p21B",
-    "p31B", "p33A", "p03A", "p13A", "aA", "t33A", "u33A", "p30B", "t23A", "u23A",
-    "p32B", "p12B", "aB", "t32B", "t10A", "u10A", "u32B", "t21B", "t13A", "t13B",
-    "t12A", "u13B", "t32A", "t22B", "t22A", "t33B", "t23B", "t31A", "t03A", "t01A",
-    "t31B", "t21A", "t10B", "t03B", "u31A", "u10B", "t12B", "t00A", "t30A", "t01B",
-    "u33B", "u22B", "u21B", "t02A", "t00B", "t02B", "u13A", "u12B", "u31B", "u03A",
-    "u32A", "u21A", "t11A", "u23B", "u11A", "u02B", "u12A", "u30A", "t20A", "t30B",
-    "t20B", "t11B", "u22A", "u11B", "u01A", "u03B", "u30B", "u02A", "u20A", "u01B",
-    "u20B", "finA", "finB",
+    "s10A", "s20A", "s10B", "s30A", "hz", "s01A", "s20B", "s03A", "hw", "hm", "s01B", "s02B",
+    "s11A", "s21A", "s33A", "s02A", "s13A", "s30B", "head", "n21A", "n10B", "s31A", "n20B", "s23A",
+    "turn", "s03B", "s22B", "s12B", "s22A", "s11B", "s12A", "n03A", "n02B", "n30A", "n11A", "n00A",
+    "n02A", "n23A", "s21B", "n01A", "m0A", "s32A", "n33A", "n31A", "n03B", "s23B", "s32B", "s31B",
+    "n01B", "n20A", "n30B", "n00B", "n22B", "m0B", "n10A", "n12B", "s13B", "n13A", "n22A", "s33B",
+    "n12A", "m2A", "m1A", "n11B", "n32A", "m3A", "aA", "n32B", "t1A", "t3A", "u31A", "u33A",
+    "n21B", "u32A", "u11A", "u13A", "n23B", "t2A", "m2B", "n31B", "u21A", "n13B", "m1B", "n33B",
+    "m3B", "aB", "t3B", "u33B", "u31B", "u32B", "t1B", "u13B", "u11B", "t0B", "t0A", "u23A",
+    "t2B", "u22A", "u01A", "u12A", "u30A", "u21B", "u23B", "u12B", "u20B", "u03B", "u03A", "u10B",
+    "u22B", "u02A", "u01B", "u10A", "u20A", "u30B", "u02B", "finA", "finB",
 )
 
 
@@ -74,6 +70,8 @@
         return i ^ 1, j
     if link == "y":
         return i ^ 2, j
+    if link == "d":
+        return i ^ 3, j
     return i, j ^ int(link[1])
 
 
@@ -82,7 +80,7 @@
     stream, docs, before, after_in, feed_in, tables, wq, wk, wv, wo,
     outs,
     slots, docs_v, before_v, after_v, feed_v, branch_v, tables_v, weights, out_weight, out_t, acc, keys, values, attended,
-    terms, shares, head, head_z, head_mid, head_plane, stats, stats_in, stats_mid, stats_zin,
+    normed, terms, shares, head, head_z, head_mid, head_plane, stats, stats_in, stats_mid, stats_zin,
     local_sem, weight_send, weight_recv, gather_send, gather_recv, reduce_send, reduce_recv,
     head_send, head_recv, stat_send, stat_recv,
 ):
@@ -93,12 +91,15 @@
     along_x, along_y, across = flip(a, 1), flip(a, 2), flip(a, 3)
     plane = (None, along_x, along_y, across)
     z_peers = [None] + [flip(b, j) for j in (1, 2, 3)]
-    peers = {"x": {"hx": along_x}, "y": {"hx": along_y}}
+    peers = {"x": {"hx": along_x}, "y": {"hx": along_y}, "d": {"hx": across}}
     for j in (1, 2, 3):
         peers["z" + str(j)] = {"hy": z_peers[j]}
 
-    def offset_of(i, j):
-        return pl.multiple_of((flip(a, i) * 4 + flip(b, j)) * width, 16)
+    def group(i):
+        return pl.multiple_of(flip(a, i) * (4 * width), 16)
+
+    def within(j):
+        return pl.multiple_of(flip(b, j) * width, 16)
 
     locals_ = [
         pltpu.make_async_copy(stream.at[:, pl.ds(0, span)], slots.at[0, 0], local_sem.at[0]),
@@ -174,7 +175,10 @@
     def share(block, h):
         k = 4 * block[0] + block[1]
         link = REDUCE["AB"[h]][k]
-        return remote(terms.at[h, k], shares.at[h, k], reduce_send.at[h, k], reduce_recv.at[h, k], peers[link])
+        return remote(
+            terms.at[h, block[0], pl.ds(within(block[1]), width)], shares.at[h, k],
+            reduce_send.at[h, k], reduce_recv.at[h, k], peers[link],
+        )
 
     blocks = [(i, j) for i in range(4) for j in range(4)]
     children = {(h, block): [] for h in range(2) for block in blocks}
@@ -235,7 +239,7 @@
         for copy in weight_remote[:3]:
             copy.wait_recv()
 
-    def project(block, h):
+    def normalise(block, h):
         await_gather(block, h)
         i, j = block
         gain_columns = state["gain_columns"]
@@ -244,12 +248,14 @@
             axis=0,
         )
         scale = state["first_scale"][:, h * span:(h + 1) * span]
-        normed = (slots[h, 4 * i + j].astype(F32) * scale * gain).astype(BF16)
+        normed[h, i, pl.ds(within(j), width), :] = (slots[h, 4 * i + j].astype(F32) * scale * gain).astype(BF16)
+
+    def project(i, h):
         part = lax.dot_general(
-            weights[pl.ds(offset_of(i, j), width), :], normed, (((0,), (0,)), ((), ())), preferred_element_type=F32
-        )
-        if ("p", h) not in arrived:
-            arrived.add(("p", h))
+            weights[pl.ds(group(i), 4 * width), :], normed[h, i], (((0,), (0,)), ((), ())), preferred_element_type=F32
+        )
+        if ("m", h) not in arrived:
+            arrived.add(("m", h))
             acc[h] = part
         else:
             acc[h] += part
@@ -302,23 +308,22 @@
             blended = jnp.dot(value, soft.astype(BF16), preferred_element_type=F32)
             attended[h, q * HEAD:(q + 1) * HEAD, :] = (blended / mass).astype(BF16)
 
-    def term(block, h):
-        at = offset_of(*block)
-        terms[h, 4 * block[0] + block[1]] = jnp.dot(
-            out_t[pl.ds(at, width), :], attended[h], preferred_element_type=F32
+    def term(i, h):
+        terms[h, i] = jnp.dot(
+            out_t[pl.ds(group(i), 4 * width), :], attended[h], preferred_element_type=F32
         ).astype(BF16)
 
     def collect(block, h):
         for child in children[h, block]:
             share(child, h).wait_recv()
-        total = terms[h, 4 * block[0] + block[1]].astype(F32)
+        total = terms[h, block[0], pl.ds(within(block[1]), width), :].astype(F32)
         for child in children[h, block]:
             total = total + shares[h, 4 * child[0] + child[1]].astype(F32)
         return total
 
     def pass_on(block, h):
         if children[h, block]:
-            terms[h, 4 * block[0] + block[1]] = collect(block, h).astype(BF16)
+            terms[h, block[0], pl.ds(within(block[1]), width), :] = collect(block, h).astype(BF16)
         share(block, h).start()
 
     def finish(h):
@@ -353,17 +358,18 @@
             finish("AB".index(task[3]))
         elif task[0] == "a":
             attend("AB".index(task[1]))
+        elif task[0] == "m":
+            project(int(task[1]), "AB".index(task[2]))
+        elif task[0] == "t":
+            term(int(task[1]), "AB".index(task[2]))
         else:
             block, h = (int(task[1]), int(task[2])), "AB".index(task[3])
             if task[0] == "s":
-                copy = gather(block, h)
                 await_gather(parent(block, GATHER["AB"[h]][4 * block[0] + block[1]]), h)
-                copy.start()
-            elif task[0] == "p":
-                project(block, h)
-            elif task[0] == "t":
-                term(block, h)
-            elif task[0] == "u":
+                gather(block, h).start()
+            elif task[0] == "n":
+                normalise(block, h)
+            else:
                 pass_on(block, h)
 
     def stat_plane(i):
@@ -439,7 +445,8 @@
             pltpu.VMEM((kcols // HEAD, HEAD, rows), BF16),
             pltpu.VMEM((kcols // HEAD, HEAD, rows), BF16),
             pltpu.VMEM((2, qcols, rows // 2), BF16),
-            pltpu.VMEM((2, 16) + piece, BF16),
+            pltpu.VMEM((2, 4, 4 * width, rows // 2), BF16),
+            pltpu.VMEM((2, 4, 4 * width, rows // 2), BF16),
             pltpu.VMEM((2, 16) + piece, BF16),
         ]
         + [pltpu.VMEM((8, rows), F32), pltpu.VMEM((3, 8, rows), F32)] * 4

time: 58.4 us -> 57.4 us (0.983)
  Pallas kernels: 55.9 us -> 54.9 us
    pallas_call x1, Pallas kernels: 55.9 us -> 54.9 us  [per_device(): pl.pallas_call(functools.partial(kernel, paired), out_shape=jax.ShapeDtyp...]
where the time goes in v2:
time: 57.4 us; the launch traced here: 57.3 us
  Pallas kernels  54.9 us (96%)
  local copies, waits for them, and re-layouts  1.71 us (3%)
  between operations  0.64 us (1%)
    pallas_call x1, Pallas kernels, per_device(): pl.pallas_call(functools.partial(kernel, paired), out_shape=jax.ShapeDtyp...  54.9 us
    transpose x1, local copies, waits for them, and re-layouts, per_device(): return (both[0].T, both[1].T)  1.71 us

profile of v2, /device:TPU:0, one launch (start us, length us, event | category | flops | bytes accessed | tf_op | source)
XLA Modules:
  0.0 57.3 jit_solution(14117280511288525080)
XLA Ops:
  0.6 54.9 %shard_map.113 = bf16[2,288,256]{2,1,0:T(8,128)(2,1)} custom-call(bf16[288,256]{1,0:T(8,128)(2,1)} %bitcast.10, s32[1,256]{1,0:T(1,128)} %bitcast.11, bf16[288]{0:T(512)(128)(2,1)} %before.1, bf16[288]{0:T(512)(128)(2,1)} %after_in.1, bf16[288]{0:T(512)(128)(2,1)} %feed_in.1, f32[2,64,256]{2,1,0:T(8,128)} %constant.2.clone.tables, bf16[2304,256]{1,0:T(8,128)(2,1)} %wq.1, ...), custom_call_target="tpu_custom_call" | custom-call | tf_op jit(solution)/shard_map/pallas_call | solution.py:428
  55.6 1.7 %slice_bitcast_fusion = (bf16[256,288]{0,1:T(8,128)(2,1)}, bf16[256,288]{0,1:T(8,128)(2,1)}) fusion(bf16[2,288,256]{2,1,0:T(8,128)(2,1)} %shard_map.113), kind=kLoop, calls=%fused_computation | loop fusion | bytes 589824 | tf_op jit(solution)/shard_map/transpose | solution.py:481

commit v3 on v2

--- a/solution.py
+++ b/solution.py
@@ -21,25 +21,26 @@
 BF16 = jnp.bfloat16
 
 
+PIECES = 1
 GATHER = {
-    "A": ("", "z1", "z1", "z3", "x", "x", "z1", "x", "y", "y", "y", "y", "d", "z1", "z1", "d"),
-    "B": ("", "z1", "z2", "z1", "x", "x", "x", "z1", "y", "y", "y", "y", "x", "z1", "x", "d"),
+    "A": ("", "z1", "z2", "z1", "x", "x", "x", "z1", "y", "y", "y", "y", "d", "x", "x", "y"),
+    "B": ("", "z1", "z2", "z1", "x", "z1", "x", "z1", "y", "z1", "y", "z1", "d", "x", "y", "d"),
 }
 REDUCE = {
-    "A": ("", "z1", "z2", "z3", "x", "x", "x", "z1", "y", "y", "y", "y", "x", "z1", "y", "x"),
-    "B": ("", "z1", "z2", "z1", "x", "x", "x", "x", "y", "y", "y", "z1", "d", "z1", "y", "x"),
+    "A": ("", "z1", "z2", "z3", "x", "z1", "x", "x", "y", "z1", "y", "y", "x", "y", "z1", "d"),
+    "B": ("", "z1", "z2", "z1", "x", "x", "x", "x", "y", "y", "y", "y", "d", "z1", "d", "z1"),
 }
 ORDER = (
-    "s10A", "s20A", "s10B", "s30A", "hz", "s01A", "s20B", "s03A", "hw", "hm", "s01B", "s02B",
-    "s11A", "s21A", "s33A", "s02A", "s13A", "s30B", "head", "n21A", "n10B", "s31A", "n20B", "s23A",
-    "turn", "s03B", "s22B", "s12B", "s22A", "s11B", "s12A", "n03A", "n02B", "n30A", "n11A", "n00A",
-    "n02A", "n23A", "s21B", "n01A", "m0A", "s32A", "n33A", "n31A", "n03B", "s23B", "s32B", "s31B",
-    "n01B", "n20A", "n30B", "n00B", "n22B", "m0B", "n10A", "n12B", "s13B", "n13A", "n22A", "s33B",
-    "n12A", "m2A", "m1A", "n11B", "n32A", "m3A", "aA", "n32B", "t1A", "t3A", "u31A", "u33A",
-    "n21B", "u32A", "u11A", "u13A", "n23B", "t2A", "m2B", "n31B", "u21A", "n13B", "m1B", "n33B",
-    "m3B", "aB", "t3B", "u33B", "u31B", "u32B", "t1B", "u13B", "u11B", "t0B", "t0A", "u23A",
-    "t2B", "u22A", "u01A", "u12A", "u30A", "u21B", "u23B", "u12B", "u20B", "u03B", "u03A", "u10B",
-    "u22B", "u02A", "u01B", "u10A", "u20A", "u30B", "u02B", "finA", "finB",
+    "s02A", "s10B", "s20A", "hz", "s01A", "s02B", "s10A", "s30B", "s30A", "s20B", "s03A", "s12A",
+    "s22A", "w0", "hw", "hm", "s21B", "s11A", "s21A", "s12B", "s13A", "s03B", "s23A", "s32A",
+    "head", "w1", "n00A", "s11B", "n30B", "n10B", "n02A", "s22B", "n11A", "turn", "s31A", "n20A",
+    "n12A", "s33A", "s01B", "n21A", "n23A", "n01A", "n03A", "n13A", "s32B", "m0A", "s31B", "n10A",
+    "n03B", "s33B", "n12B", "n22A", "n32A", "s23B", "n22B", "m1A", "m2A", "n02B", "s13B", "n31A",
+    "n11B", "n21B", "n00B", "n20B", "n30A", "n33A", "m3A", "aA", "t3A", "u32A", "u31A", "u30A",
+    "t2A", "u22A", "n32B", "t1A", "t0A", "n31B", "n23B", "u01A", "u12A", "m2B", "n01B", "m0B",
+    "u23A", "u13A", "u21A", "n33B", "n13B", "m3B", "m1B", "aB", "t3B", "u33B", "u33A", "u11A",
+    "u31B", "u02A", "t1B", "t2B", "u13B", "u12B", "u23B", "u22B", "t0B", "u32B", "u11B", "u03B",
+    "u03A", "u10A", "u10B", "u21B", "u20A", "u02B", "u20B", "u30B", "u01B", "finA", "finB",
 )
 
 
@@ -79,8 +80,8 @@
     paired,
     stream, docs, before, after_in, feed_in, tables, wq, wk, wv, wo,
     outs,
-    slots, docs_v, before_v, after_v, feed_v, branch_v, tables_v, weights, out_weight, out_t, acc, keys, values, attended,
-    normed, terms, shares, head, head_z, head_mid, head_plane, stats, stats_in, stats_mid, stats_zin,
+    slots, docs_v, before_v, after_v, feed_v, branch_v, tables_v, weights, weights_t, out_weight, out_t, acc, keys, values, attended,
+    normed, terms, shares, head, head_z, head_mid, head_plane, stats, stats_in,
     local_sem, weight_send, weight_recv, gather_send, gather_recv, reduce_send, reduce_recv,
     head_send, head_recv, stat_send, stat_recv,
 ):
@@ -96,7 +97,7 @@
         peers["z" + str(j)] = {"hy": z_peers[j]}
 
     def group(i):
-        return pl.multiple_of(flip(a, i) * (4 * width), 16)
+        return pl.multiple_of(flip(a, i) * (4 * width), LANES)
 
     def within(j):
         return pl.multiple_of(flip(b, j) * width, 16)
@@ -114,7 +115,7 @@
         copy.start()
     wrows, qcols, kcols = wq.shape[0], wq.shape[1], wk.shape[1]
     shard = c if paired else 0
-    start = pl.multiple_of(shard * wrows, 16)
+    start = pl.multiple_of(shard * wrows, LANES)
     targets = [
         (wq, weights.at[pl.ds(start, wrows), pl.ds(0, qcols)]),
         (wk, weights.at[pl.ds(start, wrows), pl.ds(qcols, kcols)]),
@@ -164,20 +165,27 @@
     def head_to_plane(i):
         return remote(head_mid, head_plane.at[i - 1], head_send.at[2 + i], head_recv.at[2 + i], {"hx": plane[i]})
 
-    def gather(block, h):
+    count = gather_send.shape[2]
+    part = width // count
+
+    def gather(block, h, f):
         link = GATHER["AB"[h]][4 * block[0] + block[1]]
         origin = parent(block, link)
-        k = 4 * block[0] + block[1]
+        k, rows_of = 4 * block[0] + block[1], pl.ds(f * part, part)
         return remote(
-            slots.at[h, 4 * origin[0] + origin[1]], slots.at[h, k], gather_send.at[h, k], gather_recv.at[h, k], peers[link]
+            slots.at[h, 4 * origin[0] + origin[1], rows_of], slots.at[h, k, rows_of],
+            gather_send.at[h, k, f], gather_recv.at[h, k, f], peers[link],
         )
 
-    def share(block, h):
+    def piece_of(block, f):
+        return pl.ds(pl.multiple_of(within(block[1]) + f * part, 16), part)
+
+    def share(block, h, f):
         k = 4 * block[0] + block[1]
         link = REDUCE["AB"[h]][k]
         return remote(
-            terms.at[h, block[0], pl.ds(within(block[1]), width)], shares.at[h, k],
-            reduce_send.at[h, k], reduce_recv.at[h, k], peers[link],
+            terms.at[h, block[0], piece_of(block, f)], shares.at[h, k, pl.ds(f * part, part)],
+            reduce_send.at[h, k, f], reduce_recv.at[h, k, f], peers[link],
         )
 
     blocks = [(i, j) for i in range(4) for j in range(4)]
@@ -196,10 +204,10 @@
     state = {}
     arrived = set()
 
-    def await_gather(block, h):
-        if block != (0, 0) and ("g", block, h) not in arrived:
-            arrived.add(("g", block, h))
-            gather(block, h).wait_recv()
+    def await_gather(block, h, f):
+        if block != (0, 0) and ("g", block, h, f) not in arrived:
+            arrived.add(("g", block, h, f))
+            gather(block, h, f).wait_recv()
 
     def send_heads():
         for j in (3, 2, 1):
@@ -234,13 +242,26 @@
         state["first_sq"] = groups[0][0:1] + groups[1][0:1] + groups[2][0:1] + groups[3][0:1]
         state["first_scale"] = lax.rsqrt(state["first_sq"] / D + epsilon)
         state["gain_columns"] = tall(jnp.concatenate(groups, axis=0))
+
+    def turn_weights(first, amount):
+        for k in range(amount // (4 * width)):
+            at = pl.ds(pl.multiple_of(first + k * 4 * width, LANES), 4 * width)
+            weights_t[:, at] = weights[at, :].T
+
+    def own_weights():
         for copy in weight_local[:3]:
             copy.wait()
+        turn_weights(start, wrows)
+
+    def other_weights():
         for copy in weight_remote[:3]:
             copy.wait_recv()
+        if paired:
+            turn_weights(pl.multiple_of((1 - c) * wrows, LANES), wrows)
 
     def normalise(block, h):
-        await_gather(block, h)
+        for f in range(count):
+            await_gather(block, h, f)
         i, j = block
         gain_columns = state["gain_columns"]
         gain = jnp.concatenate(
@@ -251,14 +272,12 @@
         normed[h, i, pl.ds(within(j), width), :] = (slots[h, 4 * i + j].astype(F32) * scale * gain).astype(BF16)
 
     def project(i, h):
-        part = lax.dot_general(
-            weights[pl.ds(group(i), 4 * width), :], normed[h, i], (((0,), (0,)), ((), ())), preferred_element_type=F32
-        )
+        product = jnp.dot(weights_t[:, pl.ds(group(i), 4 * width)], normed[h, i], preferred_element_type=F32)
         if ("m", h) not in arrived:
             arrived.add(("m", h))
-            acc[h] = part
+            acc[h] = product
         else:
-            acc[h] += part
+            acc[h] += product
 
     shards, depth, columns = out_weight.shape
 
@@ -313,41 +332,41 @@
             out_t[pl.ds(group(i), 4 * width), :], attended[h], preferred_element_type=F32
         ).astype(BF16)
 
-    def collect(block, h):
+    def collect(block, h, f):
         for child in children[h, block]:
-            share(child, h).wait_recv()
-        total = terms[h, block[0], pl.ds(within(block[1]), width), :].astype(F32)
+            share(child, h, f).wait_recv()
+        total = terms[h, block[0], piece_of(block, f), :].astype(F32)
         for child in children[h, block]:
-            total = total + shares[h, 4 * child[0] + child[1]].astype(F32)
+            total = total + shares[h, 4 * child[0] + child[1], f * part:(f + 1) * part].astype(F32)
         return total
 
-    def pass_on(block, h):
+    def pass_on(block, h, f):
         if children[h, block]:
-            terms[h, block[0], pl.ds(within(block[1]), width), :] = collect(block, h).astype(BF16)
-        share(block, h).start()
+            terms[h, block[0], piece_of(block, f), :] = collect(block, h, f).astype(BF16)
+        share(block, h, f).start()
 
     def finish(h):
-        mixed = collect((0, 0), h)
         lanes = slice(h * span, (h + 1) * span)
-        wide = slots[h, 0].astype(F32)
-        branch = mixed * state["after"]
-        narrow = row8[:, :span]
-        stats[:, lanes] = jnp.where(
-            narrow == 0,
-            jnp.sum(mixed * mixed, axis=0, keepdims=True),
-            jnp.where(
-                narrow == 1,
-                jnp.sum(wide * branch, axis=0, keepdims=True),
-                jnp.sum(branch * branch, axis=0, keepdims=True),
-            ),
-        )
-        branch_v[:, lanes] = branch
+        sums = [0.0, 0.0, 0.0]
+        for f in range(count):
+            mixed = collect((0, 0), h, f)
+            at = slice(f * part, (f + 1) * part)
+            branch = mixed * state["after"][at]
+            branch_v[at, lanes] = branch
+            for k, product in enumerate((mixed * mixed, slots[h, 0, at].astype(F32) * branch, branch * branch)):
+                sums[k] = sums[k] + jnp.sum(product, axis=0, keepdims=True)
+        row4 = lax.broadcasted_iota(jnp.int32, (4, span), 0)
+        stats[4 * h:4 * h + 4, :] = jnp.where(row4 == 0, sums[0], jnp.where(row4 == 1, sums[1], sums[2]))
 
     for task in ORDER:
         if task == "hz":
             send_heads()
         elif task == "hw":
             send_weights()
+        elif task == "w0":
+            own_weights()
+        elif task == "w1":
+            other_weights()
         elif task == "hm":
             relay_heads()
         elif task == "head":
@@ -364,40 +383,39 @@
             term(int(task[1]), "AB".index(task[2]))
         else:
             block, h = (int(task[1]), int(task[2])), "AB".index(task[3])
+            f = int(task[4]) if len(task) > 4 else 0
             if task[0] == "s":
-                await_gather(parent(block, GATHER["AB"[h]][4 * block[0] + block[1]]), h)
-                gather(block, h).start()
+                await_gather(parent(block, GATHER["AB"[h]][4 * block[0] + block[1]]), h, f)
+                gather(block, h, f).start()
             elif task[0] == "n":
                 normalise(block, h)
             else:
-                pass_on(block, h)
-
-    def stat_plane(i):
-        return remote(stats, stats_in.at[i - 1], stat_send.at[i - 1], stat_recv.at[i - 1], {"hx": plane[i]})
-
-    def stat_z(j):
-        return remote(stats_mid, stats_zin.at[j - 1], stat_send.at[2 + j], stat_recv.at[2 + j], {"hy": z_peers[j]})
-
-    for i in (3, 2, 1):
-        stat_plane(i).start()
-    for i in (1, 2, 3):
-        stat_plane(i).wait_recv()
-    stats_mid[...] = stats[...] + stats_in[0] + stats_in[1] + stats_in[2]
-    for j in (3, 2, 1):
-        stat_z(j).start()
+                pass_on(block, h, f)
+
+    def stat(i, j):
+        k = 4 * i + j
+        return remote(
+            stats, stats_in.at[k], stat_send.at[k], stat_recv.at[k], {"hx": flip(a, i), "hy": flip(b, j)}
+        )
+
+    far_first = sorted(blocks[1:], key=lambda block: -(bin(block[0]).count("1") + block[1]))
+    for block in far_first:
+        stat(*block).start()
     for h in range(2):
         for block in blocks[1:]:
-            gather(block, h).wait_send()
-            share(block, h).wait_send()
+            for f in range(count):
+                gather(block, h, f).wait_send()
+                share(block, h, f).wait_send()
     for j in (1, 2, 3):
         head_to_z(j).wait_send()
         head_to_plane(j).wait_send()
-        stat_plane(j).wait_send()
     for copy in weight_remote:
         copy.wait_send()
-    for j in (1, 2, 3):
-        stat_z(j).wait_recv()
-    summed = stats_mid[...] + stats_zin[0] + stats_zin[1] + stats_zin[2]
+    packed = stats[...]
+    for block in reversed(far_first):
+        stat(*block).wait_recv()
+        packed = packed + stats_in[4 * block[0] + block[1]]
+    summed = jnp.concatenate([packed[0:3], packed[4:7]], axis=1)
     after_scale = lax.rsqrt(summed[0:1] / D + epsilon)
     feed_sq = state["first_sq"] + 2.0 * after_scale * summed[1:2] + after_scale * after_scale * summed[2:3]
     feed_scale = lax.rsqrt(feed_sq / D + epsilon)
@@ -406,8 +424,8 @@
         residual = (slots[h, 0].astype(F32) + branch_v[:, lanes] * after_scale[:, lanes]).astype(BF16)
         outs[0, :, lanes] = residual
         outs[1, :, lanes] = (residual.astype(F32) * feed_scale[:, lanes] * state["feed"]).astype(BF16)
-    for j in (1, 2, 3):
-        stat_z(j).wait_send()
+    for block in far_first:
+        stat(*block).wait_send()
 
 
 def per_device(paired, stream_in, before_gain, after_gain, feed_gain, query_weight, key_weight, value_weight, output_weight, documents):
@@ -427,7 +445,7 @@
     block, piece = (width, rows), (width, rows // 2)
     both = pl.pallas_call(
         functools.partial(kernel, paired),
-        out_shape=jax.ShapeDtypeStruct((2,) + block, BF16),
+        out_shape=pltpu.VMEM((2,) + block, BF16),
         in_specs=[any_spec] * 10,
         out_specs=vmem,
         scratch_shapes=[
@@ -439,6 +457,7 @@
             pltpu.VMEM(block, F32),
             pltpu.VMEM((2, HEAD // 2, LENGTH), F32),
             pltpu.VMEM((D, qcols + 2 * kcols), BF16),
+            pltpu.VMEM((qcols + 2 * kcols, D), BF16),
             pltpu.VMEM((shards, depth, output_weight.shape[1]), BF16),
             pltpu.VMEM((D, depth), BF16),
             pltpu.VMEM((2, qcols + 2 * kcols, rows // 2), F32),
@@ -449,19 +468,20 @@
             pltpu.VMEM((2, 4, 4 * width, rows // 2), BF16),
             pltpu.VMEM((2, 16) + piece, BF16),
         ]
-        + [pltpu.VMEM((8, rows), F32), pltpu.VMEM((3, 8, rows), F32)] * 4
+        + [pltpu.VMEM((8, rows), F32), pltpu.VMEM((3, 8, rows), F32)] * 2
+        + [pltpu.VMEM((8, rows // 2), F32), pltpu.VMEM((16, 8, rows // 2), F32)]
         + [
             dma((11,)),
             dma((4,)),
             dma((4,)),
-            dma((2, 16)),
-            dma((2, 16)),
-            dma((2, 16)),
-            dma((2, 16)),
+            dma((2, 16, PIECES)),
+            dma((2, 16, PIECES)),
+            dma((2, 16, PIECES)),
+            dma((2, 16, PIECES)),
             dma((6,)),
             dma((6,)),
-            dma((6,)),
-            dma((6,)),
+            dma((16,)),
+            dma((16,)),
         ],
         compiler_params=pltpu.CompilerParams(
             collective_id=0, has_side_effects=True, vmem_limit_bytes=56 * 1024 * 1024

time: 57.4 us -> 53.6 us (0.934)
  Pallas kernels: 54.9 us -> 52.1 us
  local copies, waits for them, and re-layouts: 1.71 us -> 0.73 us
    pallas_call x1, Pallas kernels: 54.9 us -> 52.1 us  [per_device(): pl.pallas_call(functools.partial(kernel, paired), out_shape=pltpu.VMEM((2...]
    transpose x1, local copies, waits for them, and re-layouts: 1.71 us -> 0.73 us  [per_device(): return (both[0].T, both[1].T)]
where the time goes in v3:
time: 53.6 us; the launch traced here: 53.5 us
  Pallas kernels  52.1 us (97%)
  local copies, waits for them, and re-layouts  0.73 us (1%)
  between operations  0.64 us (1%)
    pallas_call x1, Pallas kernels, per_device(): pl.pallas_call(functools.partial(kernel, paired), out_shape=pltpu.VMEM((2...  52.1 us

profile of v3, /device:TPU:0, one launch (start us, length us, event | category | flops | bytes accessed | tf_op | source)
XLA Modules:
  0.0 53.5 jit_solution(11073029263156693527)
XLA Ops:
  0.6 52.1 %shard_map.113 = bf16[2,288,256]{2,1,0:T(8,128)(2,1)S(1)} custom-call(bf16[288,256]{1,0:T(8,128)(2,1)} %bitcast.10, s32[1,256]{1,0:T(1,128)} %bitcast.11, bf16[288]{0:T(512)(128)(2,1)} %before.1, bf16[288]{0:T(512)(128)(2,1)} %after_in.1, bf16[288]{0:T(512)(128)(2,1)} %feed_in.1, f32[2,64,256]{2,1,0:T(8,128)} %constant.2.clone.tables, bf16[2304,256]{1,0:T(8,128)(2,1)} %wq.1, ...), custom_call_target="tpu_custom_call" | custom-call | tf_op jit(solution)/shard_map/pallas_call | solution.py:446
  52.7 0.7 %slice_bitcast_fusion = (bf16[256,288]{0,1:T(8,128)(2,1)}, bf16[256,288]{0,1:T(8,128)(2,1)}) fusion(bf16[2,288,256]{2,1,0:T(8,128)(2,1)S(1)} %shard_map.113), kind=kLoop, calls=%fused_computation | loop fusion | bytes 589824 | tf_op jit(solution)/shard_map/transpose | solution.py:501

commit v4 on v3

--- a/solution.py
+++ b/solution.py
@@ -31,15 +31,15 @@
     "B": ("", "z1", "z2", "z1", "x", "x", "x", "x", "y", "y", "y", "y", "d", "z1", "d", "z1"),
 }
 ORDER = (
-    "s02A", "s10B", "s20A", "hz", "s01A", "s02B", "s10A", "s30B", "s30A", "s20B", "s03A", "s12A",
-    "s22A", "w0", "hw", "hm", "s21B", "s11A", "s21A", "s12B", "s13A", "s03B", "s23A", "s32A",
+    "s02A", "s10B", "s20A", "hz", "hw", "s01A", "s02B", "s10A", "s30B", "s30A", "s20B", "s03A",
+    "s12A", "s22A", "w0", "hm", "s21B", "s11A", "s21A", "s13A", "s12B", "s03B", "s23A", "s32A",
     "head", "w1", "n00A", "s11B", "n30B", "n10B", "n02A", "s22B", "n11A", "turn", "s31A", "n20A",
     "n12A", "s33A", "s01B", "n21A", "n23A", "n01A", "n03A", "n13A", "s32B", "m0A", "s31B", "n10A",
-    "n03B", "s33B", "n12B", "n22A", "n32A", "s23B", "n22B", "m1A", "m2A", "n02B", "s13B", "n31A",
+    "n03B", "n32A", "s23B", "s33B", "n12B", "n22A", "n22B", "m1A", "m2A", "n02B", "s13B", "n31A",
     "n11B", "n21B", "n00B", "n20B", "n30A", "n33A", "m3A", "aA", "t3A", "u32A", "u31A", "u30A",
     "t2A", "u22A", "n32B", "t1A", "t0A", "n31B", "n23B", "u01A", "u12A", "m2B", "n01B", "m0B",
     "u23A", "u13A", "u21A", "n33B", "n13B", "m3B", "m1B", "aB", "t3B", "u33B", "u33A", "u11A",
-    "u31B", "u02A", "t1B", "t2B", "u13B", "u12B", "u23B", "u22B", "t0B", "u32B", "u11B", "u03B",
+    "u31B", "u02A", "t1B", "t2B", "u13B", "u12B", "u23B", "u22B", "u32B", "t0B", "u11B", "u03B",
     "u03A", "u10A", "u10B", "u21B", "u20A", "u02B", "u20B", "u30B", "u01B", "finA", "finB",
 )
 
@@ -82,8 +82,7 @@
     outs,
     slots, docs_v, before_v, after_v, feed_v, branch_v, tables_v, weights, weights_t, out_weight, out_t, acc, keys, values, attended,
     normed, terms, shares, head, head_z, head_mid, head_plane, stats, stats_in,
-    local_sem, weight_send, weight_recv, gather_send, gather_recv, reduce_send, reduce_recv,
-    head_send, head_recv, stat_send, stat_recv,
+    local_sem, send_sem, weight_recv, gather_recv, reduce_recv, head_recv, stat_recv,
 ):
     width, rows = stream.shape
     rest = width - rows
@@ -159,13 +158,19 @@
             src_ref=src, dst_ref=dst, send_sem=send, recv_sem=recv, device_id=peer, device_id_type=MESH
         )
 
+    def arrival(ref, sem):
+        remote(ref, ref, sem, sem, {"hx": along_x}).wait_recv()
+
+    def sent(ref, sem):
+        remote(ref, ref, sem, sem, {"hx": along_x}).wait_send()
+
     def head_to_z(j):
-        return remote(head, head_z.at[j - 1], head_send.at[j - 1], head_recv.at[j - 1], {"hy": z_peers[j]})
+        return remote(head, head_z.at[j - 1], send_sem.at[2], head_recv.at[0], {"hy": z_peers[j]})
 
     def head_to_plane(i):
-        return remote(head_mid, head_plane.at[i - 1], head_send.at[2 + i], head_recv.at[2 + i], {"hx": plane[i]})
-
-    count = gather_send.shape[2]
+        return remote(head_mid, head_plane.at[i - 1], send_sem.at[3], head_recv.at[1], {"hx": plane[i]})
+
+    count = gather_recv.shape[1]
     part = width // count
 
     def gather(block, h, f):
@@ -174,7 +179,7 @@
         k, rows_of = 4 * block[0] + block[1], pl.ds(f * part, part)
         return remote(
             slots.at[h, 4 * origin[0] + origin[1], rows_of], slots.at[h, k, rows_of],
-            gather_send.at[h, k, f], gather_recv.at[h, k, f], peers[link],
+            send_sem.at[0], gather_recv.at[h * 15 + k - 1, f], peers[link],
         )
 
     def piece_of(block, f):
@@ -185,7 +190,7 @@
         link = REDUCE["AB"[h]][k]
         return remote(
             terms.at[h, block[0], piece_of(block, f)], shares.at[h, k, pl.ds(f * part, part)],
-            reduce_send.at[h, k, f], reduce_recv.at[h, k, f], peers[link],
+            send_sem.at[1], reduce_recv.at[h * 15 + k - 1, f], peers[link],
         )
 
     blocks = [(i, j) for i in range(4) for j in range(4)]
@@ -198,7 +203,7 @@
     weight_remote = []
     if paired:
         weight_remote = [
-            remote(src, dst, weight_send.at[k], weight_recv.at[k], {"tok": 1 - c})
+            remote(src, dst, send_sem.at[4], weight_recv.at[k], {"tok": 1 - c})
             for k, (src, dst) in enumerate(targets)
         ]
     state = {}
@@ -218,8 +223,7 @@
             copy.start()
 
     def relay_heads():
-        for j in (1, 2, 3):
-            head_to_z(j).wait_recv()
+        arrival(head_z, head_recv.at[0])
         mains = [head[...]] + [head_z[j] for j in range(3)]
         total = mains[0] + mains[1] + mains[2] + mains[3]
         tails = jnp.zeros((1, rows), F32)
@@ -236,8 +240,7 @@
             head_to_plane(i).start()
 
     def use_heads():
-        for i in (1, 2, 3):
-            head_to_plane(i).wait_recv()
+        arrival(head_plane, head_recv.at[1])
         groups = [head_mid[...]] + [head_plane[i] for i in range(3)]
         state["first_sq"] = groups[0][0:1] + groups[1][0:1] + groups[2][0:1] + groups[3][0:1]
         state["first_scale"] = lax.rsqrt(state["first_sq"] / D + epsilon)
@@ -395,26 +398,23 @@
     def stat(i, j):
         k = 4 * i + j
         return remote(
-            stats, stats_in.at[k], stat_send.at[k], stat_recv.at[k], {"hx": flip(a, i), "hy": flip(b, j)}
+            stats, stats_in.at[k - 1], send_sem.at[5], stat_recv.at[0], {"hx": flip(a, i), "hy": flip(b, j)}
         )
 
     far_first = sorted(blocks[1:], key=lambda block: -(bin(block[0]).count("1") + block[1]))
     for block in far_first:
         stat(*block).start()
-    for h in range(2):
-        for block in blocks[1:]:
-            for f in range(count):
-                gather(block, h, f).wait_send()
-                share(block, h, f).wait_send()
-    for j in (1, 2, 3):
-        head_to_z(j).wait_send()
-        head_to_plane(j).wait_send()
-    for copy in weight_remote:
-        copy.wait_send()
+    sent(shares.at[:, pl.ds(1, 15)], send_sem.at[0])
+    sent(shares.at[:, pl.ds(1, 15)], send_sem.at[1])
+    sent(head_z, send_sem.at[2])
+    sent(head_plane, send_sem.at[3])
+    if paired:
+        sent(weights.at[pl.ds(0, wrows)], send_sem.at[4])
+        sent(out_weight.at[0], send_sem.at[4])
+    arrival(stats_in, stat_recv.at[0])
     packed = stats[...]
-    for block in reversed(far_first):
-        stat(*block).wait_recv()
-        packed = packed + stats_in[4 * block[0] + block[1]]
+    for k in range(15):
+        packed = packed + stats_in[k]
     summed = jnp.concatenate([packed[0:3], packed[4:7]], axis=1)
     after_scale = lax.rsqrt(summed[0:1] / D + epsilon)
     feed_sq = state["first_sq"] + 2.0 * after_scale * summed[1:2] + after_scale * after_scale * summed[2:3]
@@ -424,8 +424,7 @@
         residual = (slots[h, 0].astype(F32) + branch_v[:, lanes] * after_scale[:, lanes]).astype(BF16)
         outs[0, :, lanes] = residual
         outs[1, :, lanes] = (residual.astype(F32) * feed_scale[:, lanes] * state["feed"]).astype(BF16)
-    for block in far_first:
-        stat(*block).wait_send()
+    sent(stats_in, send_sem.at[5])
 
 
 def per_device(paired, stream_in, before_gain, after_gain, feed_gain, query_weight, key_weight, value_weight, output_weight, documents):
@@ -469,19 +468,15 @@
             pltpu.VMEM((2, 16) + piece, BF16),
         ]
         + [pltpu.VMEM((8, rows), F32), pltpu.VMEM((3, 8, rows), F32)] * 2
-        + [pltpu.VMEM((8, rows // 2), F32), pltpu.VMEM((16, 8, rows // 2), F32)]
+        + [pltpu.VMEM((8, rows // 2), F32), pltpu.VMEM((15, 8, rows // 2), F32)]
         + [
             dma((11,)),
+            dma((6,)),
             dma((4,)),
-            dma((4,)),
-            dma((2, 16, PIECES)),
-            dma((2, 16, PIECES)),
-            dma((2, 16, PIECES)),
-            dma((2, 16, PIECES)),
-            dma((6,)),
-            dma((6,)),
-            dma((16,)),
-            dma((16,)),
+            dma((30, PIECES)),
+            dma((30, PIECES)),
+            dma((2,)),
+            dma((1,)),
         ],
         compiler_params=pltpu.CompilerParams(
             collective_id=0, has_side_effects=True, vmem_limit_bytes=56 * 1024 * 1024

time: 53.6 us -> 52.8 us (0.985)
  Pallas kernels: 52.1 us -> 51.2 us
    pallas_call x1, Pallas kernels: 52.1 us -> 51.2 us  [per_device(): pl.pallas_call(functools.partial(kernel, paired), out_shape=pltpu.VMEM((2...]
where the time goes in v4:
time: 52.8 us; the launch traced here: 52.6 us
  Pallas kernels  51.2 us (97%)
  local copies, waits for them, and re-layouts  0.73 us (1%)
  between operations  0.64 us (1%)
    pallas_call x1, Pallas kernels, per_device(): pl.pallas_call(functools.partial(kernel, paired), out_shape=pltpu.VMEM((2...  51.2 us

profile of v4, /device:TPU:0, one launch (start us, length us, event | category | flops | bytes accessed | tf_op | source)
XLA Modules:
  0.0 52.6 jit_solution(4266906488437793788)
XLA Ops:
  0.6 51.2 %shard_map.113 = bf16[2,288,256]{2,1,0:T(8,128)(2,1)S(1)} custom-call(bf16[288,256]{1,0:T(8,128)(2,1)} %bitcast.10, s32[1,256]{1,0:T(1,128)} %bitcast.11, bf16[288]{0:T(512)(128)(2,1)} %before.1, bf16[288]{0:T(512)(128)(2,1)} %after_in.1, bf16[288]{0:T(512)(128)(2,1)} %feed_in.1, f32[2,64,256]{2,1,0:T(8,128)} %constant.2.clone.tables, bf16[2304,256]{1,0:T(8,128)(2,1)} %wq.1, ...), custom_call_target="tpu_custom_call" | custom-call | tf_op jit(solution)/shard_map/pallas_call | solution.py:445
  51.9 0.7 %slice_bitcast_fusion = (bf16[256,288]{0,1:T(8,128)(2,1)}, bf16[256,288]{0,1:T(8,128)(2,1)}) fusion(bf16[2,288,256]{2,1,0:T(8,128)(2,1)S(1)} %shard_map.113), kind=kLoop, calls=%fused_computation | loop fusion | bytes 589824 | tf_op jit(solution)/shard_map/transpose | solution.py:496

commit v5 on v4

v5 whole, which is shorter than its diff:
```python
import functools

import jax
import jax.numpy as jnp
import numpy as np
from jax import lax
from jax.experimental import pallas as pl
from jax.experimental.pallas import tpu as pltpu
from jax.sharding import PartitionSpec as P

D = 4608
QH = 32
HEAD = 128
LENGTH = 256
LANES = 128

epsilon = 1e-06
neg_big = -1e30
MESH = pl.DeviceIdType.MESH
F32 = jnp.float32
BF16 = jnp.bfloat16


GATHER_0 = (
    (-1, 3, 4, 3, 0, 0, 0, 3, 1, 1, 1, 1, 2, 0, 0, 1),
    (-1, 3, 4, 3, 0, 3, 0, 3, 1, 3, 1, 3, 2, 0, 1, 2),
)
REDUCE_0 = (
    (-1, 3, 4, 5, 0, 3, 0, 0, 1, 3, 1, 1, 0, 1, 3, 2),
    (-1, 3, 4, 3, 0, 0, 0, 0, 1, 1, 1, 1, 2, 3, 2, 3),
)
ORDER_0 = (
    2, 20, 8, 116, 117, 1, 18, 4, 28, 12, 24, 3, 6, 10, 120, 118, 25, 5, 9, 7,
    22, 19, 11, 14, 119, 121, 32, 21, 60, 52, 34, 26, 37, 122, 13, 40, 38, 15, 17, 41,
    43, 33, 35, 39, 30, 96, 29, 36, 51, 46, 27, 31, 54, 42, 58, 97, 98, 50, 23, 45,
    53, 57, 48, 56, 44, 47, 99, 112, 107, 78, 77, 76, 106, 74, 62, 105, 104, 61, 59, 65,
    70, 102, 49, 100, 75, 71, 73, 63, 55, 103, 101, 113, 111, 95, 79, 69, 93, 66, 109, 110,
    87, 86, 91, 90, 94, 108, 85, 83, 67, 68, 84, 89, 72, 82, 88, 92, 81, 114, 115,
)
GATHER_1 = (
    (-1, 3, 3, 5, 0, 0, 0, 0, 1, 1, 3, 1, 0, 1, 3, 1),
    (-1, 3, 3, 5, 0, 0, 0, 0, 1, 3, 3, 1, 1, 2, 2, 1),
)
REDUCE_1 = (
    (-1, 3, 4, 5, 0, 0, 3, 0, 1, 1, 1, 1, 0, 3, 0, 1),
    (-1, 3, 3, 5, 0, 3, 0, 0, 1, 1, 3, 1, 2, 0, 3, 1),
)
ORDER_1 = (
    8, 20, 116, 117, 17, 24, 4, 3, 12, 1, 19, 28, 118, 29, 7, 5, 2, 11, 119, 9,
    44, 32, 25, 40, 21, 56, 120, 121, 18, 35, 52, 33, 23, 15, 27, 61, 122, 43, 10, 6,
    60, 39, 13, 36, 37, 49, 41, 34, 96, 57, 48, 50, 51, 14, 53, 100, 30, 22, 55, 47,
    26, 42, 59, 98, 31, 38, 97, 45, 46, 99, 112, 105, 106, 73, 70, 69, 62, 107, 58, 102,
    77, 79, 78, 75, 54, 63, 101, 103, 113, 111, 93, 94, 109, 86, 85, 74, 104, 108, 71, 110,
    76, 90, 95, 65, 66, 89, 82, 91, 87, 72, 68, 67, 84, 88, 92, 83, 81, 114, 115,
)
PLANS = ((GATHER_0, REDUCE_0, ORDER_0), (GATHER_1, REDUCE_1, ORDER_1))


def flip(index, mask):
    low = (index % 2 + mask % 2) % 2
    high = (index // 2 + mask // 2) % 2
    return low + 2 * high


def rope_tables():
    half = HEAD // 2
    frequency = (10000.0 ** (-np.arange(half, dtype=np.float32) / half)).astype(np.float32)
    angles = frequency[:, None] * np.arange(LENGTH, dtype=np.float32)[None, :]
    return np.stack([np.cos(angles), np.sin(angles)]).astype(np.float32)


def tall_row(row):
    return jnp.broadcast_to(row, (8, row.shape[1]))


def tall(block):
    return jnp.concatenate([block] * (LANES // block.shape[0]), axis=0).T


def parent(block, link):
    i, j = block
    return (i ^ (link + 1), j) if link < 3 else (i, j ^ (link - 2))


def kernel(
    paired,
    stream, docs, before, after_in, feed_in, tables, wq, wk, wv, wo,
    outs,
    slots, docs_v, before_v, after_v, feed_v, branch_v, tables_v, weights, weights_t, out_weight, out_t, acc, keys, values, attended,
    normed, terms, shares, head, head_z, head_mid, head_plane, stats, stats_in,
    local_sem, send_sem, weight_recv, gather_recv, reduce_recv, head_recv, stat_recv,
):
    width, rows = stream.shape
    rest = width - rows
    span = rows // 2
    a, b, c = lax.axis_index("hx"), lax.axis_index("hy"), lax.axis_index("tok")
    along_x, along_y, across = flip(a, 1), flip(a, 2), flip(a, 3)
    plane = (None, along_x, along_y, across)
    z_peers = [None] + [flip(b, j) for j in (1, 2, 3)]
    peers = [{"hx": along_x}, {"hx": along_y}, {"hx": across}] + [{"hy": z_peers[j]} for j in (1, 2, 3)]

    def group(i):
        return pl.multiple_of(flip(a, i) * (4 * width), LANES)

    def within(j):
        return pl.multiple_of(flip(b, j) * width, 16)

    locals_ = [
        pltpu.make_async_copy(stream.at[:, pl.ds(0, span)], slots.at[0, 0], local_sem.at[0]),
        pltpu.make_async_copy(stream.at[:, pl.ds(span, span)], slots.at[1, 0], local_sem.at[9]),
        pltpu.make_async_copy(before, before_v, local_sem.at[1]),
        pltpu.make_async_copy(tables, tables_v, local_sem.at[2]),
        pltpu.make_async_copy(docs, docs_v, local_sem.at[7]),
        pltpu.make_async_copy(after_in, after_v, local_sem.at[8]),
        pltpu.make_async_copy(feed_in, feed_v, local_sem.at[10]),
    ]
    for copy in locals_:
        copy.start()
    wrows, qcols, kcols = wq.shape[0], wq.shape[1], wk.shape[1]
    shard = c if paired else 0
    start = pl.multiple_of(shard * wrows, LANES)
    targets = [
        (wq, weights.at[pl.ds(start, wrows), pl.ds(0, qcols)]),
        (wk, weights.at[pl.ds(start, wrows), pl.ds(qcols, kcols)]),
        (wv, weights.at[pl.ds(start, wrows), pl.ds(qcols + kcols, kcols)]),
        (wo, out_weight.at[shard]),
    ]
    weight_local = [
        pltpu.make_async_copy(src, dst, local_sem.at[3 + k]) for k, (src, dst) in enumerate(targets)
    ]

    barrier = pltpu.get_barrier_semaphore()
    greet = [{"hx": along_x}, {"hx": along_y}, {"hx": across}]
    greet += [{"hy": z_peers[j]} for j in (1, 2, 3)]
    if paired:
        greet.append({"tok": 1 - c})
    for peer in greet:
        pl.semaphore_signal(barrier, inc=1, device_id=peer, device_id_type=MESH)
    for copy in weight_local:
        copy.start()

    row8 = lax.broadcasted_iota(jnp.int32, (8, rows), 0)
    for copy in locals_[:3]:
        copy.wait()
    own = jnp.concatenate([slots[0, 0], slots[1, 0]], axis=1).astype(F32)

    def padded(vector):
        wide_vector = vector.astype(F32).reshape(1, width)
        return jnp.concatenate([wide_vector, jnp.zeros((1, rows + LANES - width), F32)], axis=1)

    before_row = padded(before_v[...])
    padded_tail = jnp.concatenate([before_row[:, rows:], jnp.zeros((1, rows - LANES), F32)], axis=1)
    head[...] = jnp.where(
        row8 == 0,
        jnp.sum(own * own, axis=0, keepdims=True),
        jnp.where(row8 == 1, before_row[:, :rows], jnp.where(row8 == 2, padded_tail, 0.0)),
    )
    pl.semaphore_wait(barrier, len(greet))

    def run(gather_links, reduce_links, order):

        def remote(src, dst, send, recv, peer):
            return pltpu.make_async_remote_copy(
                src_ref=src, dst_ref=dst, send_sem=send, recv_sem=recv, device_id=peer, device_id_type=MESH
            )

        def arrival(ref, sem):
            remote(ref, ref, sem, sem, {"hx": along_x}).wait_recv()

        def sent(ref, sem):
            remote(ref, ref, sem, sem, {"hx": along_x}).wait_send()

        def head_to_z(j):
            return remote(head, head_z.at[j - 1], send_sem.at[2], head_recv.at[0], {"hy": z_peers[j]})

        def head_to_plane(i):
            return remote(head_mid, head_plane.at[i - 1], send_sem.at[3], head_recv.at[1], {"hx": plane[i]})

        count = gather_recv.shape[1]
        part = width // count

        def gather(block, h, f):
            link = gather_links[h][4 * block[0] + block[1]]
            origin = parent(block, link)
            k, rows_of = 4 * block[0] + block[1], pl.ds(f * part, part)
            return remote(
                slots.at[h, 4 * origin[0] + origin[1], rows_of], slots.at[h, k, rows_of],
                send_sem.at[0], gather_recv.at[h * 15 + k - 1, f], peers[link],
            )

        def piece_of(block, f):
            return pl.ds(pl.multiple_of(within(block[1]) + f * part, 16), part)

        def share(block, h, f):
            k = 4 * block[0] + block[1]
            link = reduce_links[h][k]
            return remote(
                terms.at[h, block[0], piece_of(block, f)], shares.at[h, k, pl.ds(f * part, part)],
                send_sem.at[1], reduce_recv.at[h * 15 + k - 1, f], peers[link],
            )

        blocks = [(i, j) for i in range(4) for j in range(4)]
        children = {(h, block): [] for h in range(2) for block in blocks}
        for h in range(2):
            for block in blocks[1:]:
                link = reduce_links[h][4 * block[0] + block[1]]
                children[h, parent(block, link)].append(block)

        weight_remote = []
        if paired:
            weight_remote = [
                remote(src, dst, send_sem.at[4], weight_recv.at[k], {"tok": 1 - c})
                for k, (src, dst) in enumerate(targets)
            ]
        state = {}
        arrived = set()

        def await_gather(block, h, f):
            if block != (0, 0) and ("g", block, h, f) not in arrived:
                arrived.add(("g", block, h, f))
                gather(block, h, f).wait_recv()

        def send_heads():
            for j in (3, 2, 1):
                head_to_z(j).start()

        def send_weights():
            for copy in weight_remote:
                copy.start()

        def relay_heads():
            arrival(head_z, head_recv.at[0])
            mains = [head[...]] + [head_z[j] for j in range(3)]
            total = mains[0] + mains[1] + mains[2] + mains[3]
            tails = jnp.zeros((1, rows), F32)
            for j in range(4):
                part = mains[j][2:3, :LANES]
                if j:
                    part = pltpu.roll(tall_row(part), j * rest, 1)[0:1]
                tails = tails + jnp.concatenate([part, jnp.zeros((1, rows - LANES), F32)], axis=1)
            mid = jnp.where(row8 == 0, total[0:1], 0.0)
            for j in range(4):
                mid = jnp.where(row8 == 1 + j, mains[j][1:2], mid)
            head_mid[...] = jnp.where(row8 == 5, tails, mid)
            for i in (3, 1, 2):
                head_to_plane(i).start()

        def use_heads():
            arrival(head_plane, head_recv.at[1])
            groups = [head_mid[...]] + [head_plane[i] for i in range(3)]
            state["first_sq"] = groups[0][0:1] + groups[1][0:1] + groups[2][0:1] + groups[3][0:1]
            state["first_scale"] = lax.rsqrt(state["first_sq"] / D + epsilon)
            state["gain_columns"] = tall(jnp.concatenate(groups, axis=0))

        def turn_weights(first, amount):
            for k in range(amount // (4 * width)):
                at = pl.ds(pl.multiple_of(first + k * 4 * width, LANES), 4 * width)
                weights_t[:, at] = weights[at, :].T

        def own_weights():
            for copy in weight_local[:3]:
                copy.wait()
            turn_weights(start, wrows)

        def other_weights():
            for copy in weight_remote[:3]:
                copy.wait_recv()
            if paired:
                turn_weights(pl.multiple_of((1 - c) * wrows, LANES), wrows)

        def normalise(block, h):
            for f in range(count):
                await_gather(block, h, f)
            i, j = block
            gain_columns = state["gain_columns"]
            gain = jnp.concatenate(
                [gain_columns[:, 8 * i + 1 + j:8 * i + 2 + j], gain_columns[j * rest:(j + 1) * rest, 8 * i + 5:8 * i + 6]],
                axis=0,
            )
            scale = state["first_scale"][:, h * span:(h + 1) * span]
            normed[h, i, pl.ds(within(j), width), :] = (slots[h, 4 * i + j].astype(F32) * scale * gain).astype(BF16)

        def project(i, h):
            product = jnp.dot(weights_t[:, pl.ds(group(i), 4 * width)], normed[h, i], preferred_element_type=F32)
            if ("m", h) not in arrived:
                arrived.add(("m", h))
                acc[h] = product
            else:
                acc[h] += product

        shards, depth, columns = out_weight.shape

        def turn():
            weight_local[3].wait()
            for copy in weight_remote[3:]:
                copy.wait_recv()
            for copy in locals_[3:]:
                copy.wait()
            step = 3 * LANES
            for k in range(D // step):
                s, at = (k * step) // columns, (k * step) % columns
                out_t[k * step:(k + 1) * step, :] = out_weight[s, :, at:at + step].T
            doc_row = docs_v[...].astype(F32)
            after_row = padded(after_v[...])
            state["doc_row"] = doc_row
            state["doc_col"] = tall(jnp.broadcast_to(doc_row, (8, rows)))[:, 0:1]
            feed_row = padded(feed_v[...])
            state["feed"] = tall(jnp.broadcast_to(feed_row, (8, rows + LANES)))[:width, 0:1]
            state["after"] = tall(jnp.broadcast_to(after_row, (8, rows + LANES)))[:width, 0:1]

        query_heads, key_heads = qcols // HEAD, kcols // HEAD
        ratio = query_heads // key_heads

        def attend(h):
            lanes = slice(h * span, (h + 1) * span)
            seen = (h + 1) * span
            cosine, sine = tables_v[0, :, lanes], tables_v[1, :, lanes]

            def rope(x):
                upper, lower = x[:HEAD // 2], x[HEAD // 2:]
                return jnp.concatenate([upper * cosine - lower * sine, lower * cosine + upper * sine], axis=0)

            for kv in range(key_heads):
                keys[kv, :, lanes] = rope(acc[h, qcols + kv * HEAD:qcols + (kv + 1) * HEAD]).astype(BF16)
                values[kv, :, lanes] = acc[h, qcols + kcols + kv * HEAD:qcols + kcols + (kv + 1) * HEAD].astype(BF16)
            s_index = lax.broadcasted_iota(jnp.int32, (seen, span), 0)
            t_index = lax.broadcasted_iota(jnp.int32, (seen, span), 1) + h * span
            allowed = (s_index <= t_index) & (state["doc_row"][:, lanes] == state["doc_col"][:seen])
            for q in range(query_heads):
                query = (rope(acc[h, q * HEAD:(q + 1) * HEAD]) * (D / QH) ** (-0.5)).astype(BF16)
                key, value = keys[q // ratio, :, :seen], values[q // ratio, :, :seen]
                scores = lax.dot_general(key, query, (((0,), (0,)), ((), ())), preferred_element_type=F32)
                best = jnp.max(jnp.where(allowed, scores, neg_big), axis=0, keepdims=True)
                soft = jnp.where(allowed, jnp.exp(scores - best), 0.0)
                mass = jnp.sum(soft, axis=0, keepdims=True)
                blended = jnp.dot(value, soft.astype(BF16), preferred_element_type=F32)
                attended[h, q * HEAD:(q + 1) * HEAD, :] = (blended / mass).astype(BF16)

        def term(i, h):
            terms[h, i] = jnp.dot(
                out_t[pl.ds(group(i), 4 * width), :], attended[h], preferred_element_type=F32
            ).astype(BF16)

        def collect(block, h, f):
            for child in children[h, block]:
                share(child, h, f).wait_recv()
            total = terms[h, block[0], piece_of(block, f), :].astype(F32)
            for child in children[h, block]:
                total = total + shares[h, 4 * child[0] + child[1], f * part:(f + 1) * part].astype(F32)
            return total

        def pass_on(block, h, f):
            if children[h, block]:
                terms[h, block[0], piece_of(block, f), :] = collect(block, h, f).astype(BF16)
            share(block, h, f).start()

        def finish(h):
            lanes = slice(h * span, (h + 1) * span)
            sums = [0.0, 0.0, 0.0]
            for f in range(count):
                mixed = collect((0, 0), h, f)
                at = slice(f * part, (f + 1) * part)
                branch = mixed * state["after"][at]
                branch_v[at, lanes] = branch
                for k, product in enumerate((mixed * mixed, slots[h, 0, at].astype(F32) * branch, branch * branch)):
                    sums[k] = sums[k] + jnp.sum(product, axis=0, keepdims=True)
            row4 = lax.broadcasted_iota(jnp.int32, (4, span), 0)
            stats[4 * h:4 * h + 4, :] = jnp.where(row4 == 0, sums[0], jnp.where(row4 == 1, sums[1], sums[2]))

        singles = (send_heads, send_weights, relay_heads, use_heads, own_weights, other_weights, turn)
        for task in order:
            h, k = task % 32 // 16, task % 16
            block = (k // 4, k % 4)
            if task < 32:
                await_gather(parent(block, gather_links[h][k]), h, 0)
                gather(block, h, 0).start()
            elif task < 64:
                normalise(block, h)
            elif task < 96:
                pass_on(block, h, 0)
            elif task < 104:
                project(task % 4, (task - 96) // 4)
            elif task < 112:
                term(task % 4, (task - 104) // 4)
            elif task < 114:
                attend(task - 112)
            elif task < 116:
                finish(task - 114)
            else:
                singles[task - 116]()

        def stat(i, j):
            k = 4 * i + j
            return remote(
                stats, stats_in.at[k - 1], send_sem.at[5], stat_recv.at[0], {"hx": flip(a, i), "hy": flip(b, j)}
            )

        far_first = sorted(blocks[1:], key=lambda block: -(bin(block[0]).count("1") + block[1]))
        for block in far_first:
            stat(*block).start()
        sent(shares.at[:, pl.ds(1, 15)], send_sem.at[0])
        sent(shares.at[:, pl.ds(1, 15)], send_sem.at[1])
        sent(head_z, send_sem.at[2])
        sent(head_plane, send_sem.at[3])
        if paired:
            sent(weights.at[pl.ds(0, wrows)], send_sem.at[4])
            sent(out_weight.at[0], send_sem.at[4])
        arrival(stats_in, stat_recv.at[0])
        packed = stats[...]
        for k in range(15):
            packed = packed + stats_in[k]
        summed = jnp.concatenate([packed[0:3], packed[4:7]], axis=1)
        after_scale = lax.rsqrt(summed[0:1] / D + epsilon)
        feed_sq = state["first_sq"] + 2.0 * after_scale * summed[1:2] + after_scale * after_scale * summed[2:3]
        feed_scale = lax.rsqrt(feed_sq / D + epsilon)
        for h in range(2):
            lanes = slice(h * span, (h + 1) * span)
            residual = (slots[h, 0].astype(F32) + branch_v[:, lanes] * after_scale[:, lanes]).astype(BF16)
            outs[0, :, lanes] = residual
            outs[1, :, lanes] = (residual.astype(F32) * feed_scale[:, lanes] * state["feed"]).astype(BF16)
        sent(stats_in, send_sem.at[5])

    for core in range(2):
        pl.when(c % 2 == core)(functools.partial(run, *PLANS[core]))


def per_device(paired, stream_in, before_gain, after_gain, feed_gain, query_weight, key_weight, value_weight, output_weight, documents):
    rows, width = stream_in.shape
    if not paired:
        query_weight, key_weight, value_weight = (
            lax.all_gather(piece, "tok", axis=0, tiled=True) for piece in (query_weight, key_weight, value_weight)
        )
        output_weight = lax.all_gather(output_weight, "tok", axis=1, tiled=True)
    tables = jnp.asarray(rope_tables())
    qcols, kcols = query_weight.shape[1], key_weight.shape[1]
    shards = 2 if paired else 1
    depth = output_weight.shape[0]
    any_spec = pl.BlockSpec(memory_space=pl.ANY)
    vmem = pl.BlockSpec(memory_space=pltpu.VMEM)
    dma = pltpu.SemaphoreType.DMA
    block, piece = (width, rows), (width, rows // 2)
    both = pl.pallas_call(
        functools.partial(kernel, paired),
        out_shape=pltpu.VMEM((2,) + block, BF16),
        in_specs=[any_spec] * 10,
        out_specs=vmem,
        scratch_shapes=[
            pltpu.VMEM((2, 16) + piece, BF16),
            pltpu.VMEM((1, rows), jnp.int32),
            pltpu.VMEM((width,), BF16),
            pltpu.VMEM((width,), BF16),
            pltpu.VMEM((width,), BF16),
            pltpu.VMEM(block, F32),
            pltpu.VMEM((2, HEAD // 2, LENGTH), F32),
            pltpu.VMEM((D, qcols + 2 * kcols), BF16),
            pltpu.VMEM((qcols + 2 * kcols, D), BF16),
            pltpu.VMEM((shards, depth, output_weight.shape[1]), BF16),
            pltpu.VMEM((D, depth), BF16),
            pltpu.VMEM((2, qcols + 2 * kcols, rows // 2), F32),
            pltpu.VMEM((kcols // HEAD, HEAD, rows), BF16),
            pltpu.VMEM((kcols // HEAD, HEAD, rows), BF16),
            pltpu.VMEM((2, qcols, rows // 2), BF16),
            pltpu.VMEM((2, 4, 4 * width, rows // 2), BF16),
            pltpu.VMEM((2, 4, 4 * width, rows // 2), BF16),
            pltpu.VMEM((2, 16) + piece, BF16),
        ]
        + [pltpu.VMEM((8, rows), F32), pltpu.VMEM((3, 8, rows), F32)] * 2
        + [pltpu.VMEM((8, rows // 2), F32), pltpu.VMEM((15, 8, rows // 2), F32)]
        + [
            dma((11,)),
            dma((6,)),
            dma((4,)),
            dma((30, 1)),
            dma((30, 1)),
            dma((2,)),
            dma((1,)),
        ],
        compiler_params=pltpu.CompilerParams(
            collective_id=0, has_side_effects=True, vmem_limit_bytes=56 * 1024 * 1024
        ),
    )(
        stream_in.T,
        documents.reshape(1, rows),
        before_gain,
        after_gain,
        feed_gain,
        tables,
        query_weight,
        key_weight,
        value_weight,
        output_weight,
    )
    return both[0].T, both[1].T


def solution(mesh):
    both = ("hx", "hy")
    in_specs = (
        P("tok", both),
        P(both),
        P(both),
        P(both),
        P("tok", both),
        P("tok", both),
        P("tok", both),
        P(both, "tok"),
        P("tok"),
    )
    out_specs = (P("tok", both), P("tok", both))
    paired = mesh.shape["tok"] == 2
    return jax.shard_map(
        functools.partial(per_device, paired), mesh=mesh, in_specs=in_specs, out_specs=out_specs, check_vma=False
    )
```

time: 52.8 us -> 51.7 us (0.979)
  Pallas kernels: 51.2 us -> 50.2 us
    pallas_call x1, Pallas kernels: 51.2 us -> 50.2 us  [per_device(): pl.pallas_call(functools.partial(kernel, paired), out_shape=pltpu.VMEM((2...]
where the time goes in v5:
time: 51.7 us; the launch traced here: 51.6 us
  Pallas kernels  50.2 us (97%)
  local copies, waits for them, and re-layouts  0.73 us (1%)
  between operations  0.64 us (1%)
    pallas_call x1, Pallas kernels, per_device(): pl.pallas_call(functools.partial(kernel, paired), out_shape=pltpu.VMEM((2...  50.2 us

profile of v5, /device:TPU:0, one launch (start us, length us, event | category | flops | bytes accessed | tf_op | source)
XLA Modules:
  0.0 51.6 jit_solution(13088639827645051731)
XLA Ops:
  0.6 50.2 %shard_map.113 = bf16[2,288,256]{2,1,0:T(8,128)(2,1)S(1)} custom-call(bf16[288,256]{1,0:T(8,128)(2,1)} %bitcast.10, s32[1,256]{1,0:T(1,128)} %bitcast.11, bf16[288]{0:T(512)(128)(2,1)} %before.1, bf16[288]{0:T(512)(128)(2,1)} %after_in.1, bf16[288]{0:T(512)(128)(2,1)} %feed_in.1, f32[2,64,256]{2,1,0:T(8,128)} %constant.2.clone.tables, bf16[2304,256]{1,0:T(8,128)(2,1)} %wq.1, ...), custom_call_target="tpu_custom_call" | custom-call | tf_op jit(solution)/shard_map/pallas_call | solution.py:442
  50.9 0.7 %slice_bitcast_fusion = (bf16[256,288]{0,1:T(8,128)(2,1)}, bf16[256,288]{0,1:T(8,128)(2,1)}) fusion(bf16[2,288,256]{2,1,0:T(8,128)(2,1)S(1)} %shard_map.113), kind=kLoop, calls=%fused_computation | loop fusion | bytes 589824 | tf_op jit(solution)/shard_map/transpose | solution.py:493
